TPU v7x, 32 devices: a whole 2x2x4 slice. The times are simulated.
32 devices in a mesh: row: 4 (over z), col: 8 (over y, x, core).
Axes of the slice: x: 2, y: 2, z: 4, core: 2. Of those that a mesh axis runs over, the one named last changes fastest.
Arguments:
- matrix: float32 [32, 512, 16, 1024], P(None, 'row', None, 'col'), may hold values from -150 to 150
- inverse_rest: float32 [32, 512, 14, 1024], P(None, 'row', None, 'col'), may hold values from -6 to 6
- upper_block: float32 [4, 512, 2, 1024], P(None, 'row', None, 'col'), may hold values from -6 to 6, as said below
- lower_below: float32 [4, 512, 14, 1024], P(None, 'row', None, 'col'), may hold values from -0.046875 to 0.046875
- lower_inverse: float32 [4, 512, 2048], P(None, 'row', 'col'), may hold values from -1 to 1, as said below
Outputs:
- plus_rows: float32 [4, 512, 16, 1024], P(None, 'row', None, 'col')
Inputs may be any that keep to these rules, and one draw needn't show every extreme that they name: `upper_block`: upper triangular. `lower_inverse`: unit lower triangular.
All inputs are finite; a program needn't handle non-finite values.
Results may differ from a plain program's by a relative error of at most 0.000052.
Values sent between devices are 32-bit elements; how exact they have to be, the bound alone decides.
No kernel may reach another device: no remote copies, remote signals or barrier semaphores. Data moves between devices by JAX's collectives and lax.ppermute only.
A program may use at most 256 MiB of HBM per device.

v0:
```python
import jax
import jax.numpy as jnp
from jax import lax
from jax.sharding import PartitionSpec as P


def dot_exact(left, right, form):
    return jnp.einsum(
        form, left, right, precision=lax.Precision.HIGHEST, preferred_element_type=jnp.float32
    )


def mirror(panel_rows, row_devices, col_devices, panel_cycles, blk_size):
    share_rows, col_ratio, width_all = panel_rows.shape
    sectioned = panel_rows.reshape(share_rows, col_ratio, 1, panel_cycles, row_devices, blk_size)
    sectioned = lax.all_to_all(sectioned, "row", split_axis=4, concat_axis=2, tiled=True)
    sectioned = sectioned.reshape(share_rows, col_devices, panel_cycles, blk_size)
    sectioned = lax.all_to_all(sectioned, "col", split_axis=1, concat_axis=0, tiled=True)
    return sectioned.reshape(col_devices * share_rows, panel_cycles * blk_size)


def per_device(matrix, inverse_rest, upper_block, lower_below, lower_inverse):
    row_devices = lax.axis_size("row")
    col_devices = lax.axis_size("col")
    col_ratio = col_devices // row_devices
    row_cycles, blk_size, col_cycles, blk_again = matrix.shape
    panel_cycles = lower_inverse.shape[0]
    width_all = lower_inverse.shape[2] * col_devices
    rest_local = inverse_rest.shape[2] * blk_size
    panel_col_cycles = upper_block.shape[2]
    local_rows = col_cycles * blk_size
    share_rows = local_rows // col_devices
    matrix_sq = jnp.sum(matrix * matrix)
    rest_sq = jnp.sum(inverse_rest * inverse_rest)
    matrix_total, rest_total = lax.psum((matrix_sq, rest_sq), ("row", "col"))
    below_all = lax.all_gather(lower_below, "row", axis=1, tiled=True).reshape(
        width_all, rest_local
    )
    inverse_rows = (
        inverse_rest.reshape(col_cycles, col_ratio, blk_size, rest_local)
        .transpose(0, 2, 1, 3)
        .reshape(local_rows, col_ratio, rest_local)
    )
    padded = jnp.concatenate(
        [
            upper_block,
            jnp.zeros(
                (row_cycles - panel_cycles, blk_size, panel_col_cycles, blk_size), jnp.float32
            ),
        ],
        axis=0,
    )
    upper_rows = (
        padded.reshape(col_cycles, col_ratio, blk_size, panel_col_cycles * blk_size)
        .transpose(0, 2, 1, 3)
        .reshape(local_rows, col_ratio, panel_col_cycles, 1, blk_size)
    )
    owner_mask = lax.broadcasted_iota(jnp.int32, (1, 1, 1, col_devices, 1), 3) == lax.axis_index(
        "col"
    )
    spread = jnp.where(owner_mask, upper_rows, 0.0).reshape(
        share_rows * lax.axis_size("col"), col_ratio, width_all
    )
    panel_share = lax.psum_scatter(
        spread - dot_exact(inverse_rows, below_all, "usm,tm->ust"),
        "col",
        scatter_dimension=0,
        tiled=True,
    )
    factor_rows = lax.all_gather(lower_inverse, "row", axis=1, tiled=True)
    factor_all = lax.all_gather(factor_rows, "col", axis=2, tiled=True).reshape(
        width_all, width_all
    )
    inverse_share = dot_exact(panel_share, factor_all, "ust,tw->usw")
    panel_sq = jnp.sum(inverse_share * inverse_share)
    mirrored = mirror(inverse_share, row_devices, col_devices, panel_cycles, blk_size)
    inverse_block = mirrored.reshape(col_cycles, blk_size, panel_cycles, blk_size).transpose(
        2, 3, 0, 1
    )
    panel_total = lax.psum(panel_sq, ("row", "col"))
    balance = jnp.sqrt(jnp.sqrt((rest_total + panel_total) / matrix_total))
    return 0.5 * (balance * matrix[:panel_cycles] + inverse_block / balance)


def solution(mesh):
    in_specs = (
        P(None, "row", None, "col"),
        P(None, "row", None, "col"),
        P(None, "row", None, "col"),
        P(None, "row", None, "col"),
        P(None, "row", "col"),
    )
    out_specs = P(None, "row", None, "col")
    return jax.shard_map(
        per_device, mesh=mesh, in_specs=in_specs, out_specs=out_specs, check_vma=False
    )
```

profile of v0, /device:TPU:0, one launch (start us, length us, event | category | flops | bytes accessed | tf_op | source)
XLA Modules:
  0.0 1002.6 jit_solution(8726137394494395812)
XLA Ops:
  6.5 0.0 copy-start.1
  6.5 0.0 all-gather.6.cloned.1.call-start
  6.5 0.7 all-gather.6.cloned.1.call-update
  7.3 0.0 all-gather.4.cloned.1.call-start
  7.3 0.7 all-gather.4.cloned.1.call-update
  8.0 0.0 all-gather.8.cloned.1.call-start
  8.1 49.3 %all-gather.6.cloned.1.call-done = f32[4,512,256]{2,1,0:T(8,128)} async-done(((f32[4,128,256]{2,1,0:T(8,128)}), f32[4,512,256]{2,1,0:T(8,128)}) %all-gather.6.cloned.1.call-update) | async-done | bytes 2097168 | tf_op jit(solution)/shard_map/all_gather | solution.py:70
  57.3 0.0 all-gather.8.cloned.1.call-update
  57.3 0.0 reduce-scatter.2.cloned.1.call-start
  57.4 0.0 copy-done.1
  57.4 3.9 concatenate.3
  61.3 6.6 reshape.37
  67.9 5.9 copy.22
  73.7 5.0 broadcast_in_dim.32
  78.7 7.2 copy.23
  85.9 12.9 %broadcast_in_dim.33 = f32[2048,2,2,8,128]{4,3,2,0,1:T(8,128)} broadcast(f32[2048,2,2,128]{3,2,0,1:T(2,128)} %copy.23), dimensions={0,1,2,4} | broadcast | bytes 37748736 | tf_op jit(solution)/shard_map/jit(_where)/broadcast_in_dim | solution.py:61
  98.8 35.5 %broadcast_in_dim.34 = f32[2048,2,2048]{2,0,1:T(8,128)} reshape(f32[2048,2,2,8,128]{4,3,2,0,1:T(8,128)} %broadcast_in_dim.33) | data formatting | bytes 67108864 | tf_op jit(solution)/shard_map/jit(_where)/broadcast_in_dim | solution.py:61
  134.3 27.9 %copy.24 = f32[32,128,14,128]{1,3,2,0:T(8,128)} copy(f32[32,128,14,128]{3,1,2,0:T(8,128)} %param.6) | data formatting | bytes 58720256 | tf_op args[1]
  162.2 27.8 %copy.25 = f32[16,128,2,1792]{3,1,0,2:T(8,128)} copy(f32[16,128,2,1792]{1,3,2,0:T(8,128)} %bitcast.38) | data formatting | bytes 58720256 | tf_op jit(solution)/shard_map/transpose | solution.py:41
  190.0 0.1 broadcast_bitcast_fusion
  190.1 120.1 %all-gather.4.cloned.1.call-done = f32[4,512,14,128]{3,1,2,0:T(8,128)} async-done(((f32[4,128,14,128]{3,1,2,0:T(8,128)}), f32[4,512,14,128]{3,1,2,0:T(8,128)}) %all-gather.4.cloned.1.call-update) | async-done | bytes 14680080 | tf_op jit(solution)/shard_map/all_gather | solution.py:36
  310.2 17.8 %copy.26 = f32[4,512,14,128]{1,0,3,2:T(4,128)} copy(f32[4,512,14,128]{3,1,2,0:T(8,128)} %all-gather.4.cloned.1.call-done) | data formatting | bytes 29360128 | tf_op jit(solution)/shard_map/all_gather | solution.py:36
  328.0 18.1 %reshape.48 = f32[2048,1792,1]{0,1,2:T(8,128)} reshape(f32[4,512,14,128]{1,0,3,2:T(4,128)} %copy.26) | data formatting | bytes 29360128 | tf_op jit(solution)/shard_map/reshape | solution.py:36
  346.1 203.7 %select_subtract_fusion = f32[2048,2,2048]{2,0,1:T(8,128)} fusion(f32[2048,2,2048]{2,0,1:T(8,128)} %broadcast_in_dim.34, pred[2048]{0:T(1024)(128)(4,1)S(1)} %broadcast_bitcast_fusion, f32[2048,2,1792]{2,0,1:T(8,128)} %bitcast.39, f32[2048,1792,1]{0,1,2:T(8,128)} %reshape.48), kind=kOutput, calls=%fused_computation.1 | convolution fusion | flops 180405403648 | bytes 111151104 | tf_op jit(solution)/shard_map/usm,tm->ust/dot_general | solution.py:8
  549.8 0.0 reduce-scatter.2.cloned.1.call-update
  549.8 0.0 all-gather.8.cloned.1.call-done
  549.8 203.8 %reduce-scatter.2.cloned.1.call-done = f32[256,2,2048]{2,0,1:T(8,128)} async-done(((f32[2048,2,2048]{2,0,1:T(8,128)}), f32[256,2,2048]{2,0,1:T(8,128)}) %reduce-scatter.2.cloned.1.call-update) | async-done | bytes 4194320 | tf_op jit(solution)/shard_map/reduce_scatter | solution.py:64
  753.6 34.0 %multiply_reduce_fusion.2 = (f32[]{:T(128)}, f32[256,2,2048]{2,0,1:T(8,128)}) fusion(f32[256,2,2048]{2,0,1:T(8,128)} %reduce-scatter.2.cloned.1.call-done, f32[2048,2048,1]{1,0,2:T(8,128)} %bitcast.43), kind=kOutput, calls=%fused_computation.5 | convolution fusion | flops 25771900928 | bytes 25165828 | tf_op jit(solution)/shard_map/ust,tw->usw/dot_general | solution.py:8
  787.6 6.0 reshape.42
  793.6 3.5 copy.29
  797.2 97.4 %all_to_all.24 = f32[256,2,1,4,4,128]{5,0,3,1,2,4:T(8,128)S(1)} all-to-all(f32[256,2,1,4,4,128]{5,0,3,1,2,4:T(8,128)S(1)} %copy.29), channel_id=1, replica_groups=mesh['row'=4,'col'=8] {'row'}, dimensions={4} | all-to-all | bytes 8388608 | tf_op jit(solution)/shard_map/all_to_all | solution.py:16
  894.5 2.3 copy.30
  896.8 4.5 all-to-all-start.1
  901.4 4.5 slice.3
  905.9 14.0 %multiply_reduce_fusion.1 = f32[]{:T(128)} fusion(f32[32,128,14,128]{3,1,2,0:T(8,128)} %param.6), kind=kLoop, calls=%fused_computation.2 | loop fusion | flops 14680063 | bytes 29360132 | tf_op jit(solution)/shard_map/reduce_sum | solution.py:34
  919.9 15.6 %multiply_reduce_fusion = f32[]{:T(128)} fusion(f32[32,128,16,128]{3,2,1,0:T(8,128)} %param.5), kind=kLoop, calls=%fused_computation | loop fusion | flops 16777215 | bytes 33554436 | tf_op jit(solution)/shard_map/reduce_sum | solution.py:33
  936.8 5.3 copy.35
  942.1 39.7 %all-reduce.1 = (f32[]{:T(128)}, f32[]{:T(128)}) all-reduce(f32[]{:T(128)S(6)} %add.16, f32[]{:T(128)} %multiply_reduce_fusion), channel_id=1, replica_groups=mesh['row'=4,'col'=8] {'row','col'}, use_global_device_ids=true, to_apply=%region_1.0 | all-reduce | flops 2 | bytes 16 | tf_op jit(solution)/shard_map/psum | solution.py:35
  983.1 0.0 all-to-all-done.1
  983.1 2.6 divide_bitcast_fusion
  985.7 0.0 copy-start
  985.7 0.3 copy.31
  986.0 1.9 copy-done
  987.9 2.8 add_multiply_fusion
  990.7 5.4 copy.32
  (1 shorter events, 0.0 us)
Async XLA Ops:
  6.5 50.9 %copy-start.1 = (f32[4,128,2,128]{3,2,1,0:T(2,128)S(1)}, f32[4,128,2,128]{3,2,1,0:T(2,128)}, u32[]{:S(2)}) copy-start(f32[4,128,2,128]{3,2,1,0:T(2,128)} %param.7) | copy-start | bytes 1572868
  6.5 50.8 %all-gather.6.cloned.1.call-start = ((), (), s32[]{:S(2)}) async-start(), calls=%async_computation.5 | async-start | bytes 2621440 | tf_op jit(solution)/shard_map/all_gather | solution.py:70
  7.3 302.9 %all-gather.4.cloned.1.call-start = ((), (), s32[]{:S(2)}) async-start(), calls=%async_computation.3 | async-start | bytes 18350080 | tf_op jit(solution)/shard_map/all_gather | solution.py:36
  8.0 541.8 %all-gather.8.cloned.1.call-start = ((), (), s32[]{:S(2)}) async-start(), calls=%async_computation.6 | async-start | bytes 18874368 | tf_op jit(solution)/shard_map/all_gather | solution.py:71
  57.3 696.2 %reduce-scatter.2.cloned.1.call-start = ((), (), s32[]{:S(2)}) async-start(), calls=%async_computation.4 | async-start | bytes 37748736 | tf_op jit(solution)/shard_map/reduce_scatter | solution.py:64
  896.8 86.2 %all-to-all-start.1 = ((f32[256,8,4,128]{3,0,2,1:T(8,128)}), f32[256,8,4,128]{3,0,2,1:T(8,128)}, u32[]{:S(2)}, u32[]{:S(2)}) async-start(f32[256,8,4,128]{3,0,2,1:T(8,128)} %bitcast.40), calls=%async_computation.2 | async-start | bytes 8388608 | tf_op jit(solution)/shard_map/all_to_all | solution.py:18
  985.7 2.2 copy-start
Sparse Core Ops, SparseCore 0:
  8.9 48.3 all-gather.5
  58.9 251.2 all-gather.3
  312.1 91.1 all-gather.7
  549.9 203.6 reduce-scatter.1
where the time goes:
time: 1010 us; the launch traced here: 1000 us
  waiting for transfers between devices  375 us (37%)
  matrix products  238 us (24%)
  local copies, waits for them, and re-layouts  198 us (20%)
  blocking collectives  137 us (14%)
  other arithmetic  35.1 us (3%)
  between operations  15.7 us (2%)
    dot_general x2, matrix products, dot_exact(): jnp.einsum(form, left, right, precision=lax.Precision.HIGHEST, preferred_...  238 us
    reduce_scatter x1, waiting for transfers between devices, per_device(): lax.psum_scatter(spread - dot_exact(inverse_rows, below_all, 'usm,tm->ust...  204 us
    all_gather x1, waiting for transfers between devices, per_device(): lax.all_gather(lower_below, 'row', axis=1, tiled=True)  120 us
    all_to_all x1, blocking collectives, mirror(): lax.all_to_all(sectioned, 'row', split_axis=4, concat_axis=2, tiled=True)  97.4 us
    broadcast_in_dim x5, local copies, waits for them, and re-layouts, per_device(): jnp.where(owner_mask, upper_rows, 0.0)  60.7 us
    all_gather x1, waiting for transfers between devices, per_device(): factor_rows = lax.all_gather(lower_inverse, 'row', axis=1, tiled=True)  49.3 us
    psum x1, blocking collectives, per_device(): matrix_total, rest_total = lax.psum((matrix_sq, rest_sq), ('row', 'col'))  39.7 us
    unnamed x6, local copies, waits for them, and re-layouts  35.1 us
  transfers between devices with their start and end apart: 5, of which 3 were waited for; matrix products, arithmetic and copies ran while one was open for 41% of the time, Pallas kernels for 0%

commit v1 on v0

v1 whole, which is shorter than its diff:
```python
import functools

import jax
import jax.numpy as jnp
from jax import lax
from jax.experimental import pallas as pl
from jax.experimental.pallas import tpu as pltpu
from jax.sharding import PartitionSpec as P


PARTS = 2
AHEAD = 4
LIMIT = 48 * 1024 * 1024


def dot_split(left, right, form):
    return jnp.einsum(
        form, left, right, precision=lax.Precision.HIGH, preferred_element_type=jnp.float32
    )


def after(value, token):
    return lax.optimization_barrier((value, token))[0]


def halves(value):
    high = value.astype(jnp.bfloat16)
    return high, (value - high.astype(jnp.float32)).astype(jnp.bfloat16)


def split_kernel(which_ref, rest_ref, out_ref, sum_ref):
    cycles, blk = rest_ref.shape[1], rest_ref.shape[3]
    depth = cycles * blk
    squares = jnp.zeros((8, blk), jnp.float32)
    for m in range(cycles):
        value = rest_ref[0, m]
        high, low = halves(value)
        out_ref[:, m * blk : (m + 1) * blk] = high
        out_ref[:, depth + m * blk : depth + (m + 1) * blk] = low
        squares = squares + jnp.sum((value * value).reshape(-1, 8, blk), axis=0)
    sum_ref[0] = squares


def split_rows(rest, which, group, ratio, half_rows):
    blk, cycles = rest.shape[2], rest.shape[1]
    depth = cycles * blk
    chips = ratio * half_rows
    count = chips * group

    def source(i, which_ref):
        u, qh, g = i // (half_rows * group), (i // group) % half_rows, i % group
        return (((qh * 2 + which_ref[0]) * group + g) * ratio + u, 0, 0, 0)

    return pl.pallas_call(
        split_kernel,
        grid_spec=pltpu.PrefetchScalarGridSpec(
            num_scalar_prefetch=1,
            grid=(count,),
            in_specs=[pl.BlockSpec((1, cycles, blk, blk), source)],
            out_specs=[
                pl.BlockSpec((blk, 2 * depth), lambda i, s: (i, 0)),
                pl.BlockSpec((1, 8, blk), lambda i, s: (i, 0, 0)),
            ],
        ),
        out_shape=[
            jax.ShapeDtypeStruct((count * blk, 2 * depth), jnp.bfloat16),
            jax.ShapeDtypeStruct((count, 8, blk), jnp.float32),
        ],
        compiler_params=pltpu.CompilerParams(vmem_limit_bytes=LIMIT),
        cost_estimate=pl.CostEstimate(
            flops=8 * count * blk * depth,
            bytes_accessed=8 * count * blk * depth,
            transcendentals=0,
        ),
    )(which, rest)


def product_kernel(rows, half_rows, order_ref, left_ref, upper_ref, *refs):
    blocks, (out_ref, high_ref, low_ref) = refs[:-3], refs[-3:]
    depth = high_ref.shape[1]
    blk = blocks[0].shape[1]
    parts = len(blocks) // rows
    row = order_ref[0]

    @pl.when(pl.program_id(0) == 0)
    def _():
        for step in range(rows):
            owner = lax.rem(row + rows - step, rows)
            at = pl.ds(pl.multiple_of(owner * blk, blk), blk)
            column = 0
            for p in range(parts):
                planes = blocks[step * parts + p]
                for m in range(planes.shape[0]):
                    high, low = halves(planes[m])
                    high_ref[at, column : column + blk] = high
                    low_ref[at, column : column + blk] = low
                    column += blk

    def dot(a, b):
        return lax.dot_general(
            a, b, (((1,), (1,)), ((), ())), preferred_element_type=jnp.float32
        )

    left_high, left_low = left_ref[:, :depth], left_ref[:, depth:]
    total = dot(left_high, high_ref[...])
    total += dot(left_low, high_ref[...])
    total += dot(left_high, low_ref[...])
    out_ref[0] = total

    first = lax.rem(order_ref[pl.program_id(0) + 3], half_rows) == 0

    @pl.when(jnp.logical_and(first, order_ref[2] == 1))
    def _():
        column = pl.ds(pl.multiple_of(order_ref[1] * blk, blk), blk)
        for g in range(upper_ref.shape[2]):
            at = slice(g * blk, (g + 1) * blk)
            out_ref[0, at, column] = out_ref[0, at, column] - upper_ref[0, 0, g]


def product(left, upper, layer, blocks, order, rows, chips):
    depth = left.shape[1] // 2
    span = blocks[0].shape[1] * rows
    share = left.shape[0] // chips
    whole = [pl.BlockSpec(b.shape, lambda k, s: (0, 0, 0)) for b in blocks]
    return pl.pallas_call(
        functools.partial(product_kernel, rows, rows // 2),
        grid_spec=pltpu.PrefetchScalarGridSpec(
            num_scalar_prefetch=1,
            grid=(chips,),
            in_specs=[
                pl.BlockSpec((share, 2 * depth), lambda k, s: (s[k + 3], 0)),
                pl.BlockSpec(
                    (1, 1) + upper.shape[2:],
                    lambda k, s: (layer, s[k + 3] // (rows // 2), 0, 0, 0),
                ),
            ]
            + whole,
            out_specs=pl.BlockSpec((1, share, span), lambda k, s: (k, 0, 0)),
            scratch_shapes=[
                pltpu.VMEM((span, depth), jnp.bfloat16),
                pltpu.VMEM((span, depth), jnp.bfloat16),
            ],
        ),
        out_shape=jax.ShapeDtypeStruct((chips, share, span), jnp.float32),
        compiler_params=pltpu.CompilerParams(vmem_limit_bytes=LIMIT),
        cost_estimate=pl.CostEstimate(
            flops=6 * chips * share * span * depth,
            bytes_accessed=4 * chips * share * (depth + span),
            transcendentals=0,
        ),
    )(order, left, upper, *blocks)


def partner(chip, k, chips):
    return chip ^ k if chips & (chips - 1) == 0 else (chip + k) % chips


def total_over(value, axis, count):
    if count & (count - 1):
        return lax.psum(value, axis)
    bit = 1
    while bit < count:
        value = value + lax.ppermute(value, axis, [(i, i ^ bit) for i in range(count)])
        bit *= 2
    return value


def per_device(matrix, inverse_rest, upper_block, lower_below, lower_inverse):
    rows = lax.axis_size("row")
    cols = lax.axis_size("col")
    row = lax.axis_index("row")
    col = lax.axis_index("col")
    ratio = cols // rows
    blk = matrix.shape[1]
    col_cycles = matrix.shape[2]
    panel_cycles = lower_inverse.shape[0]
    group = col_cycles // rows
    chips = cols // 2
    half_rows = rows // 2
    high, place = col // rows, col % rows
    core, chip = col % 2, col // 2
    share = group * blk
    span = rows * blk
    planes = inverse_rest.shape[2]
    cuts = [planes * p // PARTS for p in range(PARTS + 1)]
    cycles = list(reversed(range(panel_cycles)))

    ring = [(i, (i + 1) % rows) for i in range(rows)]
    flat = lower_below.transpose(0, 2, 1, 3)
    rest = inverse_rest.transpose(0, 2, 1, 3)
    sent = []
    panels = {}
    for cycle in cycles:
        held = [flat[cycle, cuts[p] : cuts[p + 1]] for p in range(PARTS)]
        panels[cycle] = list(held)
        for step in range(1, rows):
            for p in range(PARTS):
                block = held[p]
                if step == 1 and len(sent) >= AHEAD:
                    block = after(block, sent[-AHEAD])
                held[p] = lax.ppermute(block, "row", ring)
                sent.append(held[p])
                panels[cycle].append(held[p])

    factor_rows = lax.all_gather(lower_inverse, "row", axis=1, tiled=True)
    factor = lax.all_gather(factor_rows, "col", axis=0)

    left_send, squares_send = split_rows(rest, (1 - core)[None], group, ratio, half_rows)
    left_keep, squares_keep = split_rows(rest, core[None], group, ratio, half_rows)
    upper_cycles = panel_cycles // ratio
    upper = upper_block.reshape(upper_cycles, ratio, blk, -1, blk).transpose(3, 1, 0, 2, 4)
    matrix_sq = jnp.sum(matrix * matrix)
    row_early = after(row, matrix_sq)

    def order(cycle, active):
        active = jnp.logical_and(active, high == cycle % ratio).astype(jnp.int32)
        return jnp.stack(
            [row_early, place, active] + [partner(chip, k, chips) for k in range(chips)]
        )


    swap = [(i, i ^ 1) for i in range(cols)]
    gone, kept, shared = {}, {}, {}
    for cycle in cycles:
        layer = cycle // ratio
        gone = product(left_send, upper, layer, panels[cycle], order(cycle, core == 1), rows, chips)
        there = lax.ppermute(gone, "col", swap)
        kept[cycle] = product(
            left_keep, upper, layer, panels[cycle], order(cycle, core == 0), rows, chips,
        )
        shared[cycle] = [kept[cycle][0] + there[0]]
        for k in range(1, chips):
            shared[cycle].append(
                lax.ppermute(
                    kept[cycle][k] + there[k],
                    "col",
                    [(i, partner(i // 2, k, chips) * 2 + i % 2) for i in range(cols)],
                )
            )

    def mirror(out):
        arrived = []
        for k in range(rows):
            pairs = []
            for r in range(rows):
                for c in range(cols):
                    pairs.append(
                        (r * cols + c, ((c % rows + k) % rows) * cols + (c // rows) * rows + r)
                    )
            block = lax.dynamic_index_in_dim(out, (place + k) % rows, 1, keepdims=False)
            arrived.append(lax.ppermute(block, ("row", "col"), pairs))
        stacked = jnp.stack(arrived)
        ordered = [
            lax.dynamic_index_in_dim(stacked, (row - q) % rows, 0, keepdims=False)
            for q in range(rows)
        ]
        return jnp.stack(ordered, axis=2).reshape(-1, blk, col_cycles, blk)

    updates = {}
    totals = []
    results = []
    waiting = []
    width = span // factor.shape[3]
    for cycle in cycles:
        parts = shared[cycle]
        if cycle:
            parts = after(parts, kept[cycle - 1])
        total = sum(parts[1:], parts[0])
        if cycle == 0:
            total = after(total, results)
        updates[cycle] = total

        wide = factor[cycle * width : (cycle + 1) * width]
        out = jnp.zeros((), jnp.float32)
        for later in reversed(range(cycle, panel_cycles)):
            out = out + dot_split(wide[:, later], updates[later], "ctw,it->cwi")
        totals.append(jnp.sum(out * out))
        out = out.reshape(1, rows, blk, share)
        if cycle == 0:
            rest_sq = jnp.sum(squares_send) + jnp.sum(squares_keep)
            sums = jnp.stack([matrix_sq, rest_sq + sum(totals)])
            sums = jnp.broadcast_to(sums[:, None, None], (2, 8, blk))
            sums = total_over(sums, "row", rows)
            out = after(out, sums)
            sums = total_over(sums, "col", cols)
        waiting.insert(0, out)
        if cycle <= 2:
            results.insert(0, mirror(jnp.concatenate(waiting, axis=0)))
            waiting = []

    balance = jnp.sqrt(jnp.sqrt(sums[1, 0, 0] / sums[0, 0, 0]))
    mirrored = jnp.concatenate(results, axis=0)
    return 0.5 * (balance * matrix[:panel_cycles] - mirrored / balance)


def solution(mesh):
    in_specs = (
        P(None, "row", None, "col"),
        P(None, "row", None, "col"),
        P(None, "row", None, "col"),
        P(None, "row", None, "col"),
        P(None, "row", "col"),
    )
    out_specs = P(None, "row", None, "col")

    def whole(matrix, inverse_rest, upper_block, lower_below, lower_inverse):
        return jax.shard_map(
            per_device, mesh=mesh, in_specs=in_specs, out_specs=out_specs, check_vma=False
        )(matrix, inverse_rest, upper_block, lower_below, lower_inverse)

    return whole
```

time: 1010 us -> 738 us (0.73)
  matrix products: 238 us -> 28 us
  Pallas kernels: 0 us -> 176 us
  local copies, waits for them, and re-layouts: 198 us -> 23.1 us
  blocking collectives: 137 us -> 0 us
  starting transfers between devices: 4.66 us -> 112 us
  waiting for transfers between devices: 375 us -> 307 us
  other arithmetic: 35.1 us -> 59.2 us
    ppermute x0 -> x57, waiting for transfers between devices: none -> 256 us  [the longest x24 121 us: per_device(): held[p] = lax.ppermute(block, 'row', ring)]
    dot_general x2 -> x10, matrix products: 238 us -> 28 us  [dot_split(): jnp.einsum(form, left, right, precision=lax.Precision.HIGH, preferred_ele...]
    reduce_scatter x1 -> x0, waiting for transfers between devices: 204 us -> none  [per_device(): lax.psum_scatter(spread - dot_exact(inverse_rows, below_all, 'usm,tm->ust...]
    pallas_call x0 -> x10, Pallas kernels: none -> 176 us  [the longest x8 142 us: product(): pl.pallas_call(functools.partial(product_kernel, rows, rows // 2), grid_s...]
    all_gather x2 -> x1, waiting for transfers between devices: 120 us -> 0.01 us  [per_device(): factor = lax.all_gather(factor_rows, 'col', axis=0)]
    ppermute x0 -> x57, starting transfers between devices: none -> 112 us  [the longest x12 52.5 us: mirror(): arrived.append(lax.ppermute(block, ('row', 'col'), pairs))]
    all_to_all x1 -> x0, blocking collectives: 97.4 us -> none  [mirror(): lax.all_to_all(sectioned, 'row', split_axis=4, concat_axis=2, tiled=True)]
    broadcast_in_dim x5 -> x1, local copies, waits for them, and re-layouts: 60.7 us -> 0.07 us  [per_device(): sums = jnp.broadcast_to(sums[:, None, None], (2, 8, blk))]
  transfers between devices with their start and end apart: 5 -> 59, of which waited for: 3 -> 26; matrix products, arithmetic and copies ran while one was open for 41% -> 9% of each run, Pallas kernels for 0% -> 24%
where the time goes in v1:
time: 738 us; the launch traced here: 725 us
  waiting for transfers between devices  307 us (42%)
  Pallas kernels  176 us (24%)
  starting transfers between devices  112 us (15%)
  other arithmetic  59.2 us (8%)
  matrix products  28 us (4%)
  local copies, waits for them, and re-layouts  23.1 us (3%)
  between operations  19.3 us (3%)
    pallas_call x8, Pallas kernels, product(): pl.pallas_call(functools.partial(product_kernel, rows, rows // 2), grid_s...  142 us
    ppermute x24, waiting for transfers between devices, per_device(): held[p] = lax.ppermute(block, 'row', ring)  121 us
    ppermute x12, waiting for transfers between devices, per_device(): lax.ppermute(kept[cycle][k] + there[k], 'col', [(i, partner(i // 2, k, ch...  108 us
    ppermute x12, starting transfers between devices, mirror(): arrived.append(lax.ppermute(block, ('row', 'col'), pairs))  52.5 us
    all_gather x1, waiting for transfers between devices, per_device(): factor_rows = lax.all_gather(lower_inverse, 'row', axis=1, tiled=True)  50 us
    pallas_call x2, Pallas kernels, split_rows(): pl.pallas_call(split_kernel, grid_spec=pltpu.PrefetchScalarGridSpec(num_s...  34.5 us
    ppermute x5, starting transfers between devices, total_over(): lax.ppermute(value, axis, [(i, i ^ bit) for i in range(count)])  32.4 us
    dot_general x10, matrix products, dot_split(): jnp.einsum(form, left, right, precision=lax.Precision.HIGH, preferred_ele...  28 us
  transfers between devices with their start and end apart: 59, of which 26 were waited for; matrix products, arithmetic and copies ran while one was open for 9% of the time, Pallas kernels for 24%

profile of v1, /device:TPU:0, one launch (start us, length us, event | category | flops | bytes accessed | tf_op | source)
XLA Modules:
  0.0 725.0 jit_solution(253505737332798866)
XLA Ops:
  7.3 50.0 %all-gather.4.cloned.1.call-done = f32[4,512,256]{2,1,0:T(8,128)} async-done(((f32[4,128,256]{2,1,0:T(8,128)}), f32[4,512,256]{2,1,0:T(8,128)}) %all-gather.4.cloned.1.call-update) | async-done | bytes 2097168 | tf_op jit(solution)/shard_map/all_gather | solution.py:205
  57.3 2.4 slice_bitcast_fusion.20
  61.6 13.4 %collective-permute-done.refs_2_ = f32[7,128,128]{2,1,0:T(8,128)S(1)} collective-permute-done((f32[7,128,128]{2,1,0:T(8,128)S(1)}, f32[7,128,128]{2,1,0:T(8,128)S(1)}, u32[]{:S(2)}, u32[]{:S(2)}) %collective-permute-start) | collective-permute-done | bytes 458784 | tf_op jit(solution)/shard_map/ppermute | solution.py:201
  75.8 9.0 %collective-permute-done.1.refs_3_ = f32[7,128,128]{2,1,0:T(8,128)S(1)} collective-permute-done((f32[7,128,128]{2,1,0:T(8,128)S(1)}, f32[7,128,128]{2,1,0:T(8,128)S(1)}, u32[]{:S(2)}, u32[]{:S(2)}) %collective-permute-start.1) | collective-permute-done | bytes 458784 | tf_op jit(solution)/shard_map/ppermute | solution.py:201
  85.6 9.2 %collective-permute-done.2.refs_4_ = f32[7,128,128]{2,1,0:T(8,128)} collective-permute-done((f32[7,128,128]{2,1,0:T(8,128)S(1)}, f32[7,128,128]{2,1,0:T(8,128)}, u32[]{:S(2)}, u32[]{:S(2)}) %collective-permute-start.2) | collective-permute-done | bytes 458784 | tf_op jit(solution)/shard_map/ppermute | solution.py:201
  94.8 9.8 %collective-permute-done.3.refs_5_ = f32[7,128,128]{2,1,0:T(8,128)} collective-permute-done((f32[7,128,128]{2,1,0:T(8,128)S(1)}, f32[7,128,128]{2,1,0:T(8,128)}, u32[]{:S(2)}, u32[]{:S(2)}) %collective-permute-start.3) | collective-permute-done | bytes 458784 | tf_op jit(solution)/shard_map/ppermute | solution.py:201
  104.6 9.7 %collective-permute-done.10.refs_2_ = f32[7,128,128]{2,1,0:T(8,128)S(1)} collective-permute-done((f32[7,128,128]{2,1,0:T(8,128)S(1)}, f32[7,128,128]{2,1,0:T(8,128)S(1)}, u32[]{:S(2)}, u32[]{:S(2)}) %collective-permute-start.10) | collective-permute-done | bytes 458784 | tf_op jit(solution)/shard_map/ppermute | solution.py:201
  115.1 9.1 %collective-permute-done.11.refs_3_ = f32[7,128,128]{2,1,0:T(8,128)S(1)} collective-permute-done((f32[7,128,128]{2,1,0:T(8,128)S(1)}, f32[7,128,128]{2,1,0:T(8,128)S(1)}, u32[]{:S(2)}, u32[]{:S(2)}) %collective-permute-start.11) | collective-permute-done | bytes 458784 | tf_op jit(solution)/shard_map/ppermute | solution.py:201
  125.7 8.3 %collective-permute-done.12.refs_4_ = f32[7,128,128]{2,1,0:T(8,128)S(1)} collective-permute-done((f32[7,128,128]{2,1,0:T(8,128)S(1)}, f32[7,128,128]{2,1,0:T(8,128)S(1)}, u32[]{:S(2)}, u32[]{:S(2)}) %collective-permute-start.12) | collective-permute-done | bytes 458784 | tf_op jit(solution)/shard_map/ppermute | solution.py:201
  134.0 9.8 %collective-permute-done.13.refs_5_ = f32[7,128,128]{2,1,0:T(8,128)S(1)} collective-permute-done((f32[7,128,128]{2,1,0:T(8,128)S(1)}, f32[7,128,128]{2,1,0:T(8,128)S(1)}, u32[]{:S(2)}, u32[]{:S(2)}) %collective-permute-start.13) | collective-permute-done | bytes 458784 | tf_op jit(solution)/shard_map/ppermute | solution.py:201
  144.6 15.8 %multiply_reduce_fusion = f32[]{:T(128)} fusion(f32[32,128,16,128]{3,2,1,0:T(8,128)} %param.5), kind=kLoop, calls=%fused_computation | loop fusion | flops 16777215 | bytes 33554436 | tf_op jit(solution)/shard_map/reduce_sum | solution.py:212
  161.9 17.3 %shard_map.55 = (bf16[2048,3584]{1,0:T(8,128)(2,1)}, f32[16,8,128]{2,1,0:T(8,128)S(1)}) custom-call(s32[1]{0:T(128)} %bitcast.1.which_ref, f32[32,14,128,128]{3,2,1,0:T(8,128)} %bitcast.248), custom_call_target="tpu_custom_call" | custom-call | flops 29360128 | bytes 29360128 | tf_op jit(solution)/shard_map/pallas_call | solution.py:54
  179.8 17.3 %shard_map.56 = (bf16[2048,3584]{1,0:T(8,128)(2,1)}, f32[16,8,128]{2,1,0:T(8,128)S(1)}) custom-call(s32[1]{0:T(128)} %bitcast.3.which_ref, f32[32,14,128,128]{3,2,1,0:T(8,128)} %bitcast.249), custom_call_target="tpu_custom_call" | custom-call | flops 29360128 | bytes 29360128 | tf_op jit(solution)/shard_map/pallas_call | solution.py:54
  199.7 4.3 collective-permute-start.22
  208.2 16.9 %shard_map.58 = f32[4,512,512]{2,1,0:T(8,128)} custom-call(s32[7]{0:T(128)S(1)} %stack.215.order_ref, bf16[2048,3584]{1,0:T(8,128)(2,1)} %get-tuple-element.34.left_ref, f32[2,2,2,128,128]{4,3,2,1,0:T(8,128)S(1)} %bitcast.240, f32[7,128,128]{2,1,0:T(8,128)S(1)} %copy-done.4, f32[7,128,128]{2,1,0:T(8,128)S(1)} %copy-done.1, f32[7,128,128]{2,1,0:T(8,128)S(1)} %copy-done.6, ...), custom_call_target="tpu_custom_call" | custom-call | flops 11274289152 | bytes 18874368 | tf_op jit(solution)/shard_map/pallas_call | solution.py:125
  225.1 9.0 %collective-permute-done.22.refs_4_ = f32[7,128,128]{2,1,0:T(8,128)S(1)} collective-permute-done((f32[7,128,128]{2,1,0:T(8,128)}, f32[7,128,128]{2,1,0:T(8,128)S(1)}, u32[]{:S(2)}, u32[]{:S(2)}) %collective-permute-start.22) | collective-permute-done | bytes 458784 | tf_op jit(solution)/shard_map/ppermute | solution.py:201
  234.1 9.8 %collective-permute-done.23.refs_5_ = f32[7,128,128]{2,1,0:T(8,128)S(1)} collective-permute-done((f32[7,128,128]{2,1,0:T(8,128)}, f32[7,128,128]{2,1,0:T(8,128)S(1)}, u32[]{:S(2)}, u32[]{:S(2)}) %collective-permute-start.23) | collective-permute-done | bytes 458784 | tf_op jit(solution)/shard_map/ppermute | solution.py:201
  244.7 2.4 collective-permute-start.25
  247.1 16.4 %shard_map.60 = f32[4,512,512]{2,1,0:T(8,128)} custom-call(s32[7]{0:T(128)S(1)} %stack.221.order_ref, bf16[2048,3584]{1,0:T(8,128)(2,1)} %get-tuple-element.34.left_ref, f32[2,2,2,128,128]{4,3,2,1,0:T(8,128)S(1)} %bitcast.241, f32[7,128,128]{2,1,0:T(8,128)S(1)} %get-tuple-element.35.refs_0_, f32[7,128,128]{2,1,0:T(8,128)S(1)} %get-tuple-element.36.refs_1_, ...), custom_call_target="tpu_custom_call" | custom-call | flops 11274289152 | bytes 18874368 | tf_op jit(solution)/shard_map/pallas_call | solution.py:125
  263.5 9.9 %collective-permute-done.24.refs_6_ = f32[7,128,128]{2,1,0:T(8,128)S(1)} collective-permute-done((f32[7,128,128]{2,1,0:T(8,128)S(1)}, f32[7,128,128]{2,1,0:T(8,128)S(1)}, u32[]{:S(2)}, u32[]{:S(2)}) %collective-permute-start.24) | collective-permute-done | bytes 458784 | tf_op jit(solution)/shard_map/ppermute | solution.py:201
  274.1 6.9 collective-permute-done.25.refs_7_
  281.0 16.7 %shard_map.62 = f32[4,512,512]{2,1,0:T(8,128)} custom-call(s32[7]{0:T(128)S(1)} %stack.215.order_ref, bf16[2048,3584]{1,0:T(8,128)(2,1)} %get-tuple-element.34.left_ref, f32[2,2,2,128,128]{4,3,2,1,0:T(8,128)S(1)} %bitcast.242, f32[7,128,128]{2,1,0:T(8,128)S(1)} %get-tuple-element.41.refs_0_, f32[7,128,128]{2,1,0:T(8,128)S(1)} %get-tuple-element.42.refs_1_, ...), custom_call_target="tpu_custom_call" | custom-call | flops 11274289152 | bytes 18874368 | tf_op jit(solution)/shard_map/pallas_call | solution.py:125
  299.7 17.0 %shard_map.57 = f32[4,512,512]{2,1,0:T(8,128)} custom-call(s32[7]{0:T(128)S(1)} %stack.212.order_ref, bf16[2048,3584]{1,0:T(8,128)(2,1)} %get-tuple-element.33.left_ref, f32[2,2,2,128,128]{4,3,2,1,0:T(8,128)S(1)} %bitcast.243, f32[7,128,128]{2,1,0:T(8,128)S(1)} %copy-done.4, f32[7,128,128]{2,1,0:T(8,128)S(1)} %copy-done.2, f32[7,128,128]{2,1,0:T(8,128)S(1)} %copy-done.7, ...), custom_call_target="tpu_custom_call" | custom-call | flops 11274289152 | bytes 18874368 | tf_op jit(solution)/shard_map/pallas_call | solution.py:125
  316.7 5.5 collective-permute-done.35.refs_7_
  322.2 16.4 %shard_map.64 = f32[4,512,512]{2,1,0:T(8,128)} custom-call(s32[7]{0:T(128)S(1)} %stack.221.order_ref, bf16[2048,3584]{1,0:T(8,128)(2,1)} %get-tuple-element.34.left_ref, f32[2,2,2,128,128]{4,3,2,1,0:T(8,128)S(1)} %bitcast.244, f32[7,128,128]{2,1,0:T(8,128)S(1)} %get-tuple-element.47.refs_0_, f32[7,128,128]{2,1,0:T(8,128)S(1)} %get-tuple-element.48.refs_1_, ...), custom_call_target="tpu_custom_call" | custom-call | flops 11274289152 | bytes 18874368 | tf_op jit(solution)/shard_map/pallas_call | solution.py:125
  338.7 16.7 %shard_map.59 = f32[4,512,512]{2,1,0:T(8,128)} custom-call(s32[7]{0:T(128)S(1)} %stack.218.order_ref, bf16[2048,3584]{1,0:T(8,128)(2,1)} %get-tuple-element.33.left_ref, f32[2,2,2,128,128]{4,3,2,1,0:T(8,128)S(1)} %bitcast.245, f32[7,128,128]{2,1,0:T(8,128)S(1)} %get-tuple-element.35.refs_0_, f32[7,128,128]{2,1,0:T(8,128)S(1)} %get-tuple-element.36.refs_1_, ...), custom_call_target="tpu_custom_call" | custom-call | flops 11274289152 | bytes 18874368 | tf_op jit(solution)/shard_map/pallas_call | solution.py:125
  355.4 4.5 fusion.21
  363.4 16.8 %shard_map.61 = f32[4,512,512]{2,1,0:T(8,128)} custom-call(s32[7]{0:T(128)S(1)} %stack.212.order_ref, bf16[2048,3584]{1,0:T(8,128)(2,1)} %get-tuple-element.33.left_ref, f32[2,2,2,128,128]{4,3,2,1,0:T(8,128)S(1)} %bitcast.246, f32[7,128,128]{2,1,0:T(8,128)S(1)} %get-tuple-element.41.refs_0_, f32[7,128,128]{2,1,0:T(8,128)S(1)} %get-tuple-element.42.refs_1_, ...), custom_call_target="tpu_custom_call" | custom-call | flops 11274289152 | bytes 18874368 | tf_op jit(solution)/shard_map/pallas_call | solution.py:125
  380.2 4.7 fusion.15
  386.2 4.2 fusion.10
  392.0 17.2 %collective-permute-done.8 = f32[512,512]{1,0:T(8,128)} collective-permute-done((f32[512,512]{1,0:T(8,128)}, f32[512,512]{1,0:T(8,128)}, u32[]{:S(2)}, u32[]{:S(2)}) %collective-permute-start.8) | collective-permute-done | bytes 1048608 | tf_op jit(solution)/shard_map/ppermute | solution.py:234
  410.8 2.3 collective-permute-start.27
  413.2 24.9 %shard_map.63 = f32[4,512,512]{2,1,0:T(8,128)} custom-call(s32[7]{0:T(128)S(1)} %stack.218.order_ref, bf16[2048,3584]{1,0:T(8,128)(2,1)} %get-tuple-element.33.left_ref, f32[2,2,2,128,128]{4,3,2,1,0:T(8,128)S(1)} %bitcast.247, f32[7,128,128]{2,1,0:T(8,128)S(1)} %get-tuple-element.47.refs_0_, f32[7,128,128]{2,1,0:T(8,128)S(1)} %get-tuple-element.48.refs_1_, ...), custom_call_target="tpu_custom_call" | custom-call | flops 11274289152 | bytes 18874368 | tf_op jit(solution)/shard_map/pallas_call | solution.py:125
  439.6 3.5 fusion.4
  443.2 11.0 %collective-permute-done.18 = f32[512,512]{1,0:T(8,128)S(1)} collective-permute-done((f32[512,512]{1,0:T(8,128)}, f32[512,512]{1,0:T(8,128)S(1)}, u32[]{:S(2)}, u32[]{:S(2)}) %collective-permute-start.18) | collective-permute-done | bytes 1048608 | tf_op jit(solution)/shard_map/ppermute | solution.py:234
  456.5 19.7 %collective-permute-done.27 = f32[512,512]{1,0:T(8,128)} collective-permute-done((f32[512,512]{1,0:T(8,128)}, f32[512,512]{1,0:T(8,128)}, u32[]{:S(2)}, u32[]{:S(2)}) %collective-permute-start.27) | collective-permute-done | bytes 1048608 | tf_op jit(solution)/shard_map/ppermute | solution.py:234
  477.7 2.0 add_add_fusion.2
  481.4 40.1 %collective-permute-done.28 = f32[512,512]{1,0:T(8,128)S(1)} collective-permute-done((f32[512,512]{1,0:T(8,128)S(1)}, f32[512,512]{1,0:T(8,128)S(1)}, u32[]{:S(2)}, u32[]{:S(2)}) %collective-permute-start.28) | collective-permute-done | bytes 1048608 | tf_op jit(solution)/shard_map/ppermute | solution.py:234
  521.5 2.7 add_add_fusion
  524.2 19.7 %collective-permute-done.38 = f32[512,512]{1,0:T(8,128)S(1)} collective-permute-done((f32[512,512]{1,0:T(8,128)S(1)}, f32[512,512]{1,0:T(8,128)S(1)}, u32[]{:S(2)}, u32[]{:S(2)}) %collective-permute-start.38) | collective-permute-done | bytes 1048608 | tf_op jit(solution)/shard_map/ppermute | solution.py:234
  543.8 3.1 fusion.8
  547.0 2.2 fusion.19
  549.2 3.0 fusion.34
  552.2 2.2 fusion.14
  554.4 2.2 fusion.9
  556.7 3.1 fusion.30
  564.0 2.3 convolution_add_fusion.4
  566.2 3.0 fusion.27
  572.8 2.3 convolution_add_fusion.2
  575.1 14.1 %collective-permute-done.43 = f32[1,128,512]{2,1,0:T(8,128)S(1)} collective-permute-done((f32[1,128,512]{2,1,0:T(8,128)S(1)}, f32[1,128,512]{2,1,0:T(8,128)S(1)}, u32[]{:S(2)}, u32[]{:S(2)}) %collective-permute-start.43) | collective-permute-done | bytes 262176 | tf_op jit(solution)/shard_map/ppermute | solution.py:251
  589.2 35.4 %collective-permute-start.45 = (f32[2,128,512]{2,1,0:T(8,128)}, f32[2,128,512]{2,1,0:T(8,128)}, u32[]{:S(2)}, u32[]{:S(2)}) collective-permute-start(f32[2,128,512]{2,1,0:T(8,128)} %get-tuple-element.83), channel_id=1, source_target_pairs={{0,8},{1,16},{2,24},{3,0},{4,12},{5,20},{6,28},{7,4},{8,9},{9,17},... | collective-permute-start | bytes 1572872 | tf_op jit(solution)/shard_map/ppermute | solution.py:251
  626.7 3.2 convolution_add_fusion.1
  639.6 3.2 pad_maximum_fusion.1
  642.8 2.1 reshape.61
  644.9 4.4 fusion.25
  650.6 11.7 %collective-permute-start.48 = (f32[2,8,128]{2,1,0:T(8,128)S(1)}, f32[2,8,128]{2,1,0:T(8,128)S(1)}, u32[]{:S(2)}, u32[]{:S(2)}) collective-permute-start(f32[2,8,128]{2,1,0:T(8,128)S(1)} %broadcast_in_dim.14), channel_id=1, source_target_pairs={{0,8},{8,0},{16,24},{24,16},{1,9},{9,1},{17,25},{25,17},{2,10},{10... | collective-permute-start | bytes 24584 | tf_op jit(solution)/shard_map/ppermute | solution.py:163
  664.0 18.0 %collective-permute-start.49 = (f32[2,8,128]{2,1,0:T(8,128)S(1)}, f32[2,8,128]{2,1,0:T(8,128)S(1)}, u32[]{:S(2)}, u32[]{:S(2)}) collective-permute-start(f32[2,8,128]{2,1,0:T(8,128)S(1)} %broadcast_add_fusion), channel_id=1, source_target_pairs={{0,16},{8,24},{16,0},{24,8},{1,17},{9,25},{17,1},{25,9},{2,18},{10... | collective-permute-start | bytes 24584 | tf_op jit(solution)/shard_map/ppermute | solution.py:163
  684.9 2.4 collective-permute-start.56
  689.3 3.2 collective-permute-start.54
  696.2 6.0 collective-permute-done.51
  703.0 2.8 collective-permute-done.52
  708.7 2.0 pad_maximum_fusion.5
  710.7 2.6 reshape.63
  713.3 4.5 fusion.1
  (179 shorter events, 64.1 us)
Async XLA Ops:
  6.5 50.8 %all-gather.4.cloned.1.call-start = ((), (), s32[]{:S(2)}) async-start(), calls=%async_computation | async-start | bytes 2621440 | tf_op jit(solution)/shard_map/all_gather | solution.py:205
  7.3 539.7 %all-gather.6.cloned.1.call-start = ((), (), s32[]{:S(2)}) async-start(), calls=%async_computation.1 | async-start | bytes 18874368 | tf_op jit(solution)/shard_map/all_gather | solution.py:206
  59.8 100.7 %copy-start = (f32[7,128,128]{2,1,0:T(8,128)}, f32[7,128,128]{2,1,0:T(8,128)S(1)}, u32[]{:S(2)}) copy-start(f32[7,128,128]{2,1,0:T(8,128)S(1)} %get-tuple-element.76.refs_1_) | copy-start | bytes 1376260
  59.8 100.7 %copy-start.3 = (f32[7,128,128]{2,1,0:T(8,128)}, f32[7,128,128]{2,1,0:T(8,128)S(1)}, u32[]{:S(2)}) copy-start(f32[7,128,128]{2,1,0:T(8,128)S(1)} %get-tuple-element.77.refs_0_) | copy-start | bytes 1376260
  59.8 15.2 %collective-permute-start = (f32[7,128,128]{2,1,0:T(8,128)S(1)}, f32[7,128,128]{2,1,0:T(8,128)S(1)}, u32[]{:S(2)}, u32[]{:S(2)}) collective-permute-start(f32[7,128,128]{2,1,0:T(8,128)S(1)} %get-tuple-element.77.refs_0_), channel_id=1, source_target_pairs={{0,8},{8,16},{16,24},{24,0},{1,9},{9,17},{17,25},{25,1},{2,10},{10... | collective-permute-start | bytes 1376264 | tf_op jit(solution)/shard_map/ppermute | solution.py:201
  60.0 24.8 %collective-permute-start.1 = (f32[7,128,128]{2,1,0:T(8,128)S(1)}, f32[7,128,128]{2,1,0:T(8,128)S(1)}, u32[]{:S(2)}, u32[]{:S(2)}) collective-permute-start(f32[7,128,128]{2,1,0:T(8,128)S(1)} %get-tuple-element.76.refs_1_), channel_id=1, source_target_pairs={{0,8},{8,16},{16,24},{24,0},{1,9},{9,17},{17,25},{25,1},{2,10},{10... | collective-permute-start | bytes 1376264 | tf_op jit(solution)/shard_map/ppermute | solution.py:201
  75.0 19.8 %collective-permute-start.2 = (f32[7,128,128]{2,1,0:T(8,128)S(1)}, f32[7,128,128]{2,1,0:T(8,128)}, u32[]{:S(2)}, u32[]{:S(2)}) collective-permute-start(f32[7,128,128]{2,1,0:T(8,128)S(1)} %collective-permute-done.refs_2_), channel_id=1, source_target_pairs={{0,8},{8,16},{16,24},{24,0},{1,9},{9,17},{17,25},{25,1},{2,10},{10... | collective-permute-start | bytes 1376264 | tf_op jit(solution)/shard_map/ppermute | solution.py:201
  84.8 19.8 %collective-permute-start.3 = (f32[7,128,128]{2,1,0:T(8,128)S(1)}, f32[7,128,128]{2,1,0:T(8,128)}, u32[]{:S(2)}, u32[]{:S(2)}) collective-permute-start(f32[7,128,128]{2,1,0:T(8,128)S(1)} %collective-permute-done.1.refs_3_), channel_id=1, source_target_pairs={{0,8},{8,16},{16,24},{24,0},{1,9},{9,17},{17,25},{25,1},{2,10},{10... | collective-permute-start | bytes 1376264 | tf_op jit(solution)/shard_map/ppermute | solution.py:201
  94.8 19.6 %collective-permute-start.10 = (f32[7,128,128]{2,1,0:T(8,128)S(1)}, f32[7,128,128]{2,1,0:T(8,128)S(1)}, u32[]{:S(2)}, u32[]{:S(2)}) collective-permute-start(f32[7,128,128]{2,1,0:T(8,128)S(1)} %get-tuple-element.35.refs_0_), channel_id=1, source_target_pairs={{0,8},{8,16},{16,24},{24,0},{1,9},{9,17},{17,25},{25,1},{2,10},{10... | collective-permute-start | bytes 1376264 | tf_op jit(solution)/shard_map/ppermute | solution.py:201
  104.6 19.6 %collective-permute-start.11 = (f32[7,128,128]{2,1,0:T(8,128)S(1)}, f32[7,128,128]{2,1,0:T(8,128)S(1)}, u32[]{:S(2)}, u32[]{:S(2)}) collective-permute-start(f32[7,128,128]{2,1,0:T(8,128)S(1)} %get-tuple-element.36.refs_1_), channel_id=1, source_target_pairs={{0,8},{8,16},{16,24},{24,0},{1,9},{9,17},{17,25},{25,1},{2,10},{10... | collective-permute-start | bytes 1376264 | tf_op jit(solution)/shard_map/ppermute | solution.py:201
  114.3 19.7 %collective-permute-start.12 = (f32[7,128,128]{2,1,0:T(8,128)S(1)}, f32[7,128,128]{2,1,0:T(8,128)S(1)}, u32[]{:S(2)}, u32[]{:S(2)}) collective-permute-start(f32[7,128,128]{2,1,0:T(8,128)S(1)} %collective-permute-done.10.refs_2_), channel_id=1, source_target_pairs={{0,8},{8,16},{16,24},{24,0},{1,9},{9,17},{17,25},{25,1},{2,10},{10... | collective-permute-start | bytes 1376264 | tf_op jit(solution)/shard_map/ppermute | solution.py:201
  124.2 19.7 %collective-permute-start.13 = (f32[7,128,128]{2,1,0:T(8,128)S(1)}, f32[7,128,128]{2,1,0:T(8,128)S(1)}, u32[]{:S(2)}, u32[]{:S(2)}) collective-permute-start(f32[7,128,128]{2,1,0:T(8,128)S(1)} %collective-permute-done.11.refs_3_), channel_id=1, source_target_pairs={{0,8},{8,16},{16,24},{24,0},{1,9},{9,17},{17,25},{25,1},{2,10},{10... | collective-permute-start | bytes 1376264 | tf_op jit(solution)/shard_map/ppermute | solution.py:201
  124.9 74.1 %collective-permute-start.4 = (f32[7,128,128]{2,1,0:T(8,128)}, f32[7,128,128]{2,1,0:T(8,128)}, u32[]{:S(2)}, u32[]{:S(2)}) collective-permute-start(f32[7,128,128]{2,1,0:T(8,128)} %collective-permute-done.2.refs_4_), channel_id=1, source_target_pairs={{0,8},{8,16},{16,24},{24,0},{1,9},{9,17},{17,25},{25,1},{2,10},{10... | collective-permute-start | bytes 1376264 | tf_op jit(solution)/shard_map/ppermute | solution.py:201
  124.9 79.1 %collective-permute-start.5 = (f32[7,128,128]{2,1,0:T(8,128)}, f32[7,128,128]{2,1,0:T(8,128)}, u32[]{:S(2)}, u32[]{:S(2)}) collective-permute-start(f32[7,128,128]{2,1,0:T(8,128)} %collective-permute-done.3.refs_5_), channel_id=1, source_target_pairs={{0,8},{8,16},{16,24},{24,0},{1,9},{9,17},{17,25},{25,1},{2,10},{10... | collective-permute-start | bytes 1376264 | tf_op jit(solution)/shard_map/ppermute | solution.py:201
  134.0 65.7 %collective-permute-start.20 = (f32[7,128,128]{2,1,0:T(8,128)S(1)}, f32[7,128,128]{2,1,0:T(8,128)}, u32[]{:S(2)}, u32[]{:S(2)}) collective-permute-start(f32[7,128,128]{2,1,0:T(8,128)S(1)} %get-tuple-element.41.refs_0_), channel_id=1, source_target_pairs={{0,8},{8,16},{16,24},{24,0},{1,9},{9,17},{17,25},{25,1},{2,10},{10... | collective-permute-start | bytes 1376264 | tf_op jit(solution)/shard_map/ppermute | solution.py:201
  144.6 59.4 %collective-permute-start.21 = (f32[7,128,128]{2,1,0:T(8,128)S(1)}, f32[7,128,128]{2,1,0:T(8,128)}, u32[]{:S(2)}, u32[]{:S(2)}) collective-permute-start(f32[7,128,128]{2,1,0:T(8,128)S(1)} %get-tuple-element.42.refs_1_), channel_id=1, source_target_pairs={{0,8},{8,16},{16,24},{24,0},{1,9},{9,17},{17,25},{25,1},{2,10},{10... | collective-permute-start | bytes 1376264 | tf_op jit(solution)/shard_map/ppermute | solution.py:201
  199.0 45.0 %collective-permute-start.14 = (f32[7,128,128]{2,1,0:T(8,128)}, f32[7,128,128]{2,1,0:T(8,128)S(1)}, u32[]{:S(2)}, u32[]{:S(2)}) collective-permute-start(f32[7,128,128]{2,1,0:T(8,128)} %copy-done.15), channel_id=1, source_target_pairs={{0,8},{8,16},{16,24},{24,0},{1,9},{9,17},{17,25},{25,1},{2,10},{10... | collective-permute-start | bytes 1376264 | tf_op jit(solution)/shard_map/ppermute | solution.py:201
  199.1 45.6 %collective-permute-start.15 = (f32[7,128,128]{2,1,0:T(8,128)}, f32[7,128,128]{2,1,0:T(8,128)S(1)}, u32[]{:S(2)}, u32[]{:S(2)}) collective-permute-start(f32[7,128,128]{2,1,0:T(8,128)} %copy-done.17), channel_id=1, source_target_pairs={{0,8},{8,16},{16,24},{24,0},{1,9},{9,17},{17,25},{25,1},{2,10},{10... | collective-permute-start | bytes 1376264 | tf_op jit(solution)/shard_map/ppermute | solution.py:201
  199.7 34.4 %collective-permute-start.22 = (f32[7,128,128]{2,1,0:T(8,128)}, f32[7,128,128]{2,1,0:T(8,128)S(1)}, u32[]{:S(2)}, u32[]{:S(2)}) collective-permute-start(f32[7,128,128]{2,1,0:T(8,128)} %collective-permute-done.20.refs_2_), channel_id=1, source_target_pairs={{0,8},{8,16},{16,24},{24,0},{1,9},{9,17},{17,25},{25,1},{2,10},{10... | collective-permute-start | bytes 1376264 | tf_op jit(solution)/shard_map/ppermute | solution.py:201
  204.0 39.9 %collective-permute-start.23 = (f32[7,128,128]{2,1,0:T(8,128)}, f32[7,128,128]{2,1,0:T(8,128)S(1)}, u32[]{:S(2)}, u32[]{:S(2)}) collective-permute-start(f32[7,128,128]{2,1,0:T(8,128)} %collective-permute-done.21.refs_3_), channel_id=1, source_target_pairs={{0,8},{8,16},{16,24},{24,0},{1,9},{9,17},{17,25},{25,1},{2,10},{10... | collective-permute-start | bytes 1376264 | tf_op jit(solution)/shard_map/ppermute | solution.py:201
  208.1 38.9 %copy-start.14 = (f32[7,128,128]{2,1,0:T(8,128)S(1)}, f32[7,128,128]{2,1,0:T(8,128)}, u32[]{:S(2)}) copy-start(f32[7,128,128]{2,1,0:T(8,128)} %copy-done.13) | copy-start | bytes 1376260
  208.1 38.9 %copy-start.16 = (f32[7,128,128]{2,1,0:T(8,128)S(1)}, f32[7,128,128]{2,1,0:T(8,128)}, u32[]{:S(2)}) copy-start(f32[7,128,128]{2,1,0:T(8,128)} %copy-done.15) | copy-start | bytes 1376260
  208.2 38.9 %copy-start.18 = (f32[7,128,128]{2,1,0:T(8,128)S(1)}, f32[7,128,128]{2,1,0:T(8,128)}, u32[]{:S(2)}) copy-start(f32[7,128,128]{2,1,0:T(8,128)} %copy-done.17) | copy-start | bytes 1376260
  225.1 130.3 %collective-permute-start.6 = (f32[4,512,512]{2,1,0:T(8,128)}, f32[4,512,512]{2,1,0:T(8,128)}, u32[]{:S(2)}, u32[]{:S(2)}) collective-permute-start(f32[4,512,512]{2,1,0:T(8,128)} %shard_map.58), channel_id=1, source_target_pairs={{0,1},{1,0},{2,3},{3,2},{4,5},{5,4},{6,7},{7,6},{8,9},{9,8},{10,11... | collective-permute-start | bytes 12582920 | tf_op jit(solution)/shard_map/ppermute | solution.py:227
  234.1 39.3 %collective-permute-start.30 = (f32[7,128,128]{2,1,0:T(8,128)S(1)}, f32[7,128,128]{2,1,0:T(8,128)S(1)}, u32[]{:S(2)}, u32[]{:S(2)}) collective-permute-start(f32[7,128,128]{2,1,0:T(8,128)S(1)} %get-tuple-element.47.refs_0_), channel_id=1, source_target_pairs={{0,8},{8,16},{16,24},{24,0},{1,9},{9,17},{17,25},{25,1},{2,10},{10... | collective-permute-start | bytes 1376264 | tf_op jit(solution)/shard_map/ppermute | solution.py:201
  243.9 29.5 %collective-permute-start.31 = (f32[7,128,128]{2,1,0:T(8,128)S(1)}, f32[7,128,128]{2,1,0:T(8,128)S(1)}, u32[]{:S(2)}, u32[]{:S(2)}) collective-permute-start(f32[7,128,128]{2,1,0:T(8,128)S(1)} %get-tuple-element.48.refs_1_), channel_id=1, source_target_pairs={{0,8},{8,16},{16,24},{24,0},{1,9},{9,17},{17,25},{25,1},{2,10},{10... | collective-permute-start | bytes 1376264 | tf_op jit(solution)/shard_map/ppermute | solution.py:201
  243.9 29.5 %collective-permute-start.24 = (f32[7,128,128]{2,1,0:T(8,128)S(1)}, f32[7,128,128]{2,1,0:T(8,128)S(1)}, u32[]{:S(2)}, u32[]{:S(2)}) collective-permute-start(f32[7,128,128]{2,1,0:T(8,128)S(1)} %collective-permute-done.22.refs_4_), channel_id=1, source_target_pairs={{0,8},{8,16},{16,24},{24,0},{1,9},{9,17},{17,25},{25,1},{2,10},{10... | collective-permute-start | bytes 1376264 | tf_op jit(solution)/shard_map/ppermute | solution.py:201
  244.7 36.3 %collective-permute-start.25 = (f32[7,128,128]{2,1,0:T(8,128)S(1)}, f32[7,128,128]{2,1,0:T(8,128)S(1)}, u32[]{:S(2)}, u32[]{:S(2)}) collective-permute-start(f32[7,128,128]{2,1,0:T(8,128)S(1)} %collective-permute-done.23.refs_5_), channel_id=1, source_target_pairs={{0,8},{8,16},{16,24},{24,0},{1,9},{9,17},{17,25},{25,1},{2,10},{10... | collective-permute-start | bytes 1376264 | tf_op jit(solution)/shard_map/ppermute | solution.py:201
  273.4 89.5 %collective-permute-start.16 = (f32[4,512,512]{2,1,0:T(8,128)}, f32[4,512,512]{2,1,0:T(8,128)}, u32[]{:S(2)}, u32[]{:S(2)}) collective-permute-start(f32[4,512,512]{2,1,0:T(8,128)} %shard_map.60), channel_id=1, source_target_pairs={{0,1},{1,0},{2,3},{3,2},{4,5},{5,4},{6,7},{7,6},{8,9},{9,8},{10,11... | collective-permute-start | bytes 12582920 | tf_op jit(solution)/shard_map/ppermute | solution.py:227
  273.4 24.2 %collective-permute-start.32 = (f32[7,128,128]{2,1,0:T(8,128)S(1)}, f32[7,128,128]{2,1,0:T(8,128)S(1)}, u32[]{:S(2)}, u32[]{:S(2)}) collective-permute-start(f32[7,128,128]{2,1,0:T(8,128)S(1)} %collective-permute-done.30.refs_2_), channel_id=1, source_target_pairs={{0,8},{8,16},{16,24},{24,0},{1,9},{9,17},{17,25},{25,1},{2,10},{10... | collective-permute-start | bytes 1376264 | tf_op jit(solution)/shard_map/ppermute | solution.py:201
  273.4 25.9 %collective-permute-start.33 = (f32[7,128,128]{2,1,0:T(8,128)S(1)}, f32[7,128,128]{2,1,0:T(8,128)S(1)}, u32[]{:S(2)}, u32[]{:S(2)}) collective-permute-start(f32[7,128,128]{2,1,0:T(8,128)S(1)} %collective-permute-done.31.refs_3_), channel_id=1, source_target_pairs={{0,8},{8,16},{16,24},{24,0},{1,9},{9,17},{17,25},{25,1},{2,10},{10... | collective-permute-start | bytes 1376264 | tf_op jit(solution)/shard_map/ppermute | solution.py:201
  297.7 87.3 %collective-permute-start.26 = (f32[4,512,512]{2,1,0:T(8,128)}, f32[4,512,512]{2,1,0:T(8,128)}, u32[]{:S(2)}, u32[]{:S(2)}) collective-permute-start(f32[4,512,512]{2,1,0:T(8,128)} %shard_map.62), channel_id=1, source_target_pairs={{0,1},{1,0},{2,3},{3,2},{4,5},{5,4},{6,7},{7,6},{8,9},{9,8},{10,11... | collective-permute-start | bytes 12582920 | tf_op jit(solution)/shard_map/ppermute | solution.py:227
  297.7 19.0 %collective-permute-start.34 = (f32[7,128,128]{2,1,0:T(8,128)S(1)}, f32[7,128,128]{2,1,0:T(8,128)S(1)}, u32[]{:S(2)}, u32[]{:S(2)}) collective-permute-start(f32[7,128,128]{2,1,0:T(8,128)S(1)} %collective-permute-done.32.refs_4_), channel_id=1, source_target_pairs={{0,8},{8,16},{16,24},{24,0},{1,9},{9,17},{17,25},{25,1},{2,10},{10... | collective-permute-start | bytes 1376264 | tf_op jit(solution)/shard_map/ppermute | solution.py:201
  299.3 22.9 %collective-permute-start.35 = (f32[7,128,128]{2,1,0:T(8,128)S(1)}, f32[7,128,128]{2,1,0:T(8,128)S(1)}, u32[]{:S(2)}, u32[]{:S(2)}) collective-permute-start(f32[7,128,128]{2,1,0:T(8,128)S(1)} %collective-permute-done.33.refs_5_), channel_id=1, source_target_pairs={{0,8},{8,16},{16,24},{24,0},{1,9},{9,17},{17,25},{25,1},{2,10},{10... | collective-permute-start | bytes 1376264 | tf_op jit(solution)/shard_map/ppermute | solution.py:201
  338.7 99.5 %collective-permute-start.36 = (f32[4,512,512]{2,1,0:T(8,128)}, f32[4,512,512]{2,1,0:T(8,128)}, u32[]{:S(2)}, u32[]{:S(2)}) collective-permute-start(f32[4,512,512]{2,1,0:T(8,128)} %shard_map.64), channel_id=1, source_target_pairs={{0,1},{1,0},{2,3},{3,2},{4,5},{5,4},{6,7},{7,6},{8,9},{9,8},{10,11... | collective-permute-start | bytes 12582920 | tf_op jit(solution)/shard_map/ppermute | solution.py:227
  359.9 30.5 %collective-permute-start.7 = (f32[512,512]{1,0:T(8,128)}, f32[512,512]{1,0:T(8,128)S(1)}, u32[]{:S(2)}, u32[]{:S(2)}) collective-permute-start(f32[512,512]{1,0:T(8,128)} %get-tuple-element.68), channel_id=1, source_target_pairs={{0,2},{1,3},{2,0},{3,1},{4,6},{5,7},{6,4},{7,5},{8,10},{9,11},{10,... | collective-permute-start | bytes 3145736 | tf_op jit(solution)/shard_map/ppermute | solution.py:234
  361.4 47.9 %collective-permute-start.8 = (f32[512,512]{1,0:T(8,128)}, f32[512,512]{1,0:T(8,128)}, u32[]{:S(2)}, u32[]{:S(2)}) collective-permute-start(f32[512,512]{1,0:T(8,128)} %get-tuple-element.67), channel_id=1, source_target_pairs={{0,4},{1,5},{2,6},{3,7},{4,0},{5,1},{6,2},{7,3},{8,12},{9,13},{10,... | collective-permute-start | bytes 3145736 | tf_op jit(solution)/shard_map/ppermute | solution.py:234
  362.9 48.0 %collective-permute-start.9 = (f32[512,512]{1,0:T(8,128)}, f32[512,512]{1,0:T(8,128)}, u32[]{:S(2)}, u32[]{:S(2)}) collective-permute-start(f32[512,512]{1,0:T(8,128)} %get-tuple-element.66), channel_id=1, source_target_pairs={{0,6},{1,7},{2,4},{3,5},{4,2},{5,3},{6,0},{7,1},{8,14},{9,15},{10,... | collective-permute-start | bytes 3145736 | tf_op jit(solution)/shard_map/ppermute | solution.py:234
  384.9 53.2 %collective-permute-start.17 = (f32[512,512]{1,0:T(8,128)}, f32[512,512]{1,0:T(8,128)S(1)}, u32[]{:S(2)}, u32[]{:S(2)}) collective-permute-start(f32[512,512]{1,0:T(8,128)} %get-tuple-element.64), channel_id=1, source_target_pairs={{0,2},{1,3},{2,0},{3,1},{4,6},{5,7},{6,4},{7,5},{8,10},{9,11},{10,... | collective-permute-start | bytes 3145736 | tf_op jit(solution)/shard_map/ppermute | solution.py:234
  390.4 63.7 %collective-permute-start.18 = (f32[512,512]{1,0:T(8,128)}, f32[512,512]{1,0:T(8,128)S(1)}, u32[]{:S(2)}, u32[]{:S(2)}) collective-permute-start(f32[512,512]{1,0:T(8,128)} %get-tuple-element.63), channel_id=1, source_target_pairs={{0,4},{1,5},{2,6},{3,7},{4,0},{5,1},{6,2},{7,3},{8,12},{9,13},{10,... | collective-permute-start | bytes 3145736 | tf_op jit(solution)/shard_map/ppermute | solution.py:234
  409.2 46.3 %collective-permute-start.19 = (f32[512,512]{1,0:T(8,128)S(1)}, f32[512,512]{1,0:T(8,128)}, u32[]{:S(2)}, u32[]{:S(2)}) collective-permute-start(f32[512,512]{1,0:T(8,128)S(1)} %get-tuple-element.62), channel_id=1, source_target_pairs={{0,6},{1,7},{2,4},{3,5},{4,2},{5,3},{6,0},{7,1},{8,14},{9,15},{10,... | collective-permute-start | bytes 3145736 | tf_op jit(solution)/shard_map/ppermute | solution.py:234
  410.8 65.4 %collective-permute-start.27 = (f32[512,512]{1,0:T(8,128)}, f32[512,512]{1,0:T(8,128)}, u32[]{:S(2)}, u32[]{:S(2)}) collective-permute-start(f32[512,512]{1,0:T(8,128)} %get-tuple-element.60), channel_id=1, source_target_pairs={{0,2},{1,3},{2,0},{3,1},{4,6},{5,7},{6,4},{7,5},{8,10},{9,11},{10,... | collective-permute-start | bytes 3145736 | tf_op jit(solution)/shard_map/ppermute | solution.py:234
  438.1 83.4 %collective-permute-start.28 = (f32[512,512]{1,0:T(8,128)S(1)}, f32[512,512]{1,0:T(8,128)S(1)}, u32[]{:S(2)}, u32[]{:S(2)}) collective-permute-start(f32[512,512]{1,0:T(8,128)S(1)} %get-tuple-element.59), channel_id=1, source_target_pairs={{0,4},{1,5},{2,6},{3,7},{4,0},{5,1},{6,2},{7,3},{8,12},{9,13},{10,... | collective-permute-start | bytes 3145736 | tf_op jit(solution)/shard_map/ppermute | solution.py:234
  438.2 83.3 %collective-permute-start.29 = (f32[512,512]{1,0:T(8,128)S(1)}, f32[512,512]{1,0:T(8,128)S(1)}, u32[]{:S(2)}, u32[]{:S(2)}) collective-permute-start(f32[512,512]{1,0:T(8,128)S(1)} %get-tuple-element.58), channel_id=1, source_target_pairs={{0,6},{1,7},{2,4},{3,5},{4,2},{5,3},{6,0},{7,1},{8,14},{9,15},{10,... | collective-permute-start | bytes 3145736 | tf_op jit(solution)/shard_map/ppermute | solution.py:234
  454.2 70.0 %collective-permute-start.39 = (f32[512,512]{1,0:T(8,128)S(1)}, f32[512,512]{1,0:T(8,128)S(1)}, u32[]{:S(2)}, u32[]{:S(2)}) collective-permute-start(f32[512,512]{1,0:T(8,128)S(1)} %get-tuple-element.56), channel_id=1, source_target_pairs={{0,6},{1,7},{2,4},{3,5},{4,2},{5,3},{6,0},{7,1},{8,14},{9,15},{10,... | collective-permute-start | bytes 3145736 | tf_op jit(solution)/shard_map/ppermute | solution.py:234
  455.5 88.3 %collective-permute-start.38 = (f32[512,512]{1,0:T(8,128)S(1)}, f32[512,512]{1,0:T(8,128)S(1)}, u32[]{:S(2)}, u32[]{:S(2)}) collective-permute-start(f32[512,512]{1,0:T(8,128)S(1)} %get-tuple-element.57), channel_id=1, source_target_pairs={{0,4},{1,5},{2,6},{3,7},{4,0},{5,1},{6,2},{7,3},{8,12},{9,13},{10,... | collective-permute-start | bytes 3145736 | tf_op jit(solution)/shard_map/ppermute | solution.py:234
  476.2 67.6 %collective-permute-start.37 = (f32[512,512]{1,0:T(8,128)S(1)}, f32[512,512]{1,0:T(8,128)S(1)}, u32[]{:S(2)}, u32[]{:S(2)}) collective-permute-start(f32[512,512]{1,0:T(8,128)S(1)} %get-tuple-element.55), channel_id=1, source_target_pairs={{0,2},{1,3},{2,0},{3,1},{4,6},{5,7},{6,4},{7,5},{8,10},{9,11},{10,... | collective-permute-start | bytes 3145736 | tf_op jit(solution)/shard_map/ppermute | solution.py:234
  560.9 75.3 %collective-permute-start.47 = (f32[2,128,512]{2,1,0:T(8,128)}, f32[2,128,512]{2,1,0:T(8,128)}, u32[]{:S(2)}, u32[]{:S(2)}) collective-permute-start(f32[2,128,512]{2,1,0:T(8,128)} %get-tuple-element.85), channel_id=1, source_target_pairs={{0,24},{1,0},{2,8},{3,16},{4,28},{5,4},{6,12},{7,20},{8,25},{9,1},... | collective-permute-start | bytes 1572872 | tf_op jit(solution)/shard_map/ppermute | solution.py:251
  562.5 73.7 %collective-permute-start.46 = (f32[2,128,512]{2,1,0:T(8,128)}, f32[2,128,512]{2,1,0:T(8,128)}, u32[]{:S(2)}, u32[]{:S(2)}) collective-permute-start(f32[2,128,512]{2,1,0:T(8,128)} %get-tuple-element.84), channel_id=1, source_target_pairs={{0,16},{1,24},{2,0},{3,8},{4,20},{5,28},{6,4},{7,12},{8,17},{9,25}... | collective-permute-start | bytes 1572872 | tf_op jit(solution)/shard_map/ppermute | solution.py:251
  569.3 19.8 %collective-permute-start.43 = (f32[1,128,512]{2,1,0:T(8,128)S(1)}, f32[1,128,512]{2,1,0:T(8,128)S(1)}, u32[]{:S(2)}, u32[]{:S(2)}) collective-permute-start(f32[1,128,512]{2,1,0:T(8,128)S(1)} %get-tuple-element.99), channel_id=1, source_target_pairs={{0,24},{1,0},{2,8},{3,16},{4,28},{5,4},{6,12},{7,20},{8,25},{9,1},... | collective-permute-start | bytes 786440 | tf_op jit(solution)/shard_map/ppermute | solution.py:251
  569.4 55.2 %collective-permute-start.42 = (f32[1,128,512]{2,1,0:T(8,128)S(1)}, f32[1,128,512]{2,1,0:T(8,128)S(1)}, u32[]{:S(2)}, u32[]{:S(2)}) collective-permute-start(f32[1,128,512]{2,1,0:T(8,128)S(1)} %get-tuple-element.100), channel_id=1, source_target_pairs={{0,16},{1,24},{2,0},{3,8},{4,20},{5,28},{6,4},{7,12},{8,17},{9,25}... | collective-permute-start | bytes 786440 | tf_op jit(solution)/shard_map/ppermute | solution.py:251
  571.1 54.9 %collective-permute-start.41 = (f32[1,128,512]{2,1,0:T(8,128)S(1)}, f32[1,128,512]{2,1,0:T(8,128)S(1)}, u32[]{:S(2)}, u32[]{:S(2)}) collective-permute-start(f32[1,128,512]{2,1,0:T(8,128)S(1)} %get-tuple-element.101), channel_id=1, source_target_pairs={{0,8},{1,16},{2,24},{3,0},{4,12},{5,20},{6,28},{7,4},{8,9},{9,17},... | collective-permute-start | bytes 786440 | tf_op jit(solution)/shard_map/ppermute | solution.py:251
  589.2 47.0 %collective-permute-start.45 = (f32[2,128,512]{2,1,0:T(8,128)}, f32[2,128,512]{2,1,0:T(8,128)}, u32[]{:S(2)}, u32[]{:S(2)}) collective-permute-start(f32[2,128,512]{2,1,0:T(8,128)} %get-tuple-element.83), channel_id=1, source_target_pairs={{0,8},{1,16},{2,24},{3,0},{4,12},{5,20},{6,28},{7,4},{8,9},{9,17},... | collective-permute-start | bytes 1572872 | tf_op jit(solution)/shard_map/ppermute | solution.py:251
  624.6 11.6 %collective-permute-start.44 = (f32[2,128,512]{2,1,0:T(8,128)S(1)}, f32[2,128,512]{2,1,0:T(8,128)}, u32[]{:S(2)}, u32[]{:S(2)}) collective-permute-start(f32[2,128,512]{2,1,0:T(8,128)S(1)} %get-tuple-element.82), channel_id=1, source_target_pairs={{0,0},{1,8},{2,16},{3,24},{4,4},{5,12},{6,20},{7,28},{8,1},{9,9},{... | collective-permute-start | bytes 1572872 | tf_op jit(solution)/shard_map/ppermute | solution.py:251
  626.0 5.8 collective-permute-start.40
  650.6 13.3 %collective-permute-start.48 = (f32[2,8,128]{2,1,0:T(8,128)S(1)}, f32[2,8,128]{2,1,0:T(8,128)S(1)}, u32[]{:S(2)}, u32[]{:S(2)}) collective-permute-start(f32[2,8,128]{2,1,0:T(8,128)S(1)} %broadcast_in_dim.14), channel_id=1, source_target_pairs={{0,8},{8,0},{16,24},{24,16},{1,9},{9,1},{17,25},{25,17},{2,10},{10... | collective-permute-start | bytes 24584 | tf_op jit(solution)/shard_map/ppermute | solution.py:163
  664.0 19.6 %collective-permute-start.49 = (f32[2,8,128]{2,1,0:T(8,128)S(1)}, f32[2,8,128]{2,1,0:T(8,128)S(1)}, u32[]{:S(2)}, u32[]{:S(2)}) collective-permute-start(f32[2,8,128]{2,1,0:T(8,128)S(1)} %broadcast_add_fusion), channel_id=1, source_target_pairs={{0,16},{8,24},{16,0},{24,8},{1,17},{9,25},{17,1},{25,9},{2,18},{10... | collective-permute-start | bytes 24584 | tf_op jit(solution)/shard_map/ppermute | solution.py:163
  684.9 22.8 %collective-permute-start.56 = (f32[1,128,512]{2,1,0:T(8,128)S(1)}, f32[1,128,512]{2,1,0:T(8,128)S(1)}, u32[]{:S(2)}, u32[]{:S(2)}) collective-permute-start(f32[1,128,512]{2,1,0:T(8,128)S(1)} %get-tuple-element.91), channel_id=1, source_target_pairs={{0,24},{1,0},{2,8},{3,16},{4,28},{5,4},{6,12},{7,20},{8,25},{9,1},... | collective-permute-start | bytes 786440 | tf_op jit(solution)/shard_map/ppermute | solution.py:251
  687.3 20.4 %collective-permute-start.55 = (f32[1,128,512]{2,1,0:T(8,128)S(1)}, f32[1,128,512]{2,1,0:T(8,128)S(1)}, u32[]{:S(2)}, u32[]{:S(2)}) collective-permute-start(f32[1,128,512]{2,1,0:T(8,128)S(1)} %get-tuple-element.92), channel_id=1, source_target_pairs={{0,16},{1,24},{2,0},{3,8},{4,20},{5,28},{6,4},{7,12},{8,17},{9,25}... | collective-permute-start | bytes 786440 | tf_op jit(solution)/shard_map/ppermute | solution.py:251
  689.3 18.5 %collective-permute-start.54 = (f32[1,128,512]{2,1,0:T(8,128)S(1)}, f32[1,128,512]{2,1,0:T(8,128)S(1)}, u32[]{:S(2)}, u32[]{:S(2)}) collective-permute-start(f32[1,128,512]{2,1,0:T(8,128)S(1)} %get-tuple-element.93), channel_id=1, source_target_pairs={{0,8},{1,16},{2,24},{3,0},{4,12},{5,20},{6,28},{7,4},{8,9},{9,17},... | collective-permute-start | bytes 786440 | tf_op jit(solution)/shard_map/ppermute | solution.py:251
  692.5 15.3 %collective-permute-start.53 = (f32[1,128,512]{2,1,0:T(8,128)S(1)}, f32[1,128,512]{2,1,0:T(8,128)S(1)}, u32[]{:S(2)}, u32[]{:S(2)}) collective-permute-start(f32[1,128,512]{2,1,0:T(8,128)S(1)} %get-tuple-element.90), channel_id=1, source_target_pairs={{0,0},{1,8},{2,16},{3,24},{4,4},{5,12},{6,20},{7,28},{8,1},{9,9},{... | collective-permute-start | bytes 786440 | tf_op jit(solution)/shard_map/ppermute | solution.py:251
  693.4 2.2 collective-permute-start.50
  695.6 6.6 collective-permute-start.51
  702.2 3.7 collective-permute-start.52
  (20 other events, 221.2 us)
Sparse Core Ops, SparseCore 0:
  8.9 48.3 all-gather.3
  59.2 88.5 all-gather.5

commit v2 on v1

--- a/solution.py
+++ b/solution.py
@@ -9,14 +9,9 @@
 
 
 PARTS = 2
+HALVED = 1
 AHEAD = 4
 LIMIT = 48 * 1024 * 1024
-
-
-def dot_split(left, right, form):
-    return jnp.einsum(
-        form, left, right, precision=lax.Precision.HIGH, preferred_element_type=jnp.float32
-    )
 
 
 def after(value, token):
@@ -75,21 +70,21 @@
     )(which, rest)
 
 
-def product_kernel(rows, half_rows, order_ref, left_ref, upper_ref, *refs):
+def product_kernel(rows, half_rows, whole, order_ref, left_ref, upper_ref, *refs):
     blocks, (out_ref, high_ref, low_ref) = refs[:-3], refs[-3:]
     depth = high_ref.shape[1]
     blk = blocks[0].shape[1]
-    parts = len(blocks) // rows
+    count = len(blocks) // PARTS
     row = order_ref[0]
 
     @pl.when(pl.program_id(0) == 0)
     def _():
-        for step in range(rows):
-            owner = lax.rem(row + rows - step, rows)
+        for step in range(count):
+            owner = lax.rem(row + rows - step, rows) if whole else step
             at = pl.ds(pl.multiple_of(owner * blk, blk), blk)
             column = 0
-            for p in range(parts):
-                planes = blocks[step * parts + p]
+            for p in range(PARTS):
+                planes = blocks[step * PARTS + p]
                 for m in range(planes.shape[0]):
                     high, low = halves(planes[m])
                     high_ref[at, column : column + blk] = high
@@ -119,11 +114,12 @@
 
 def product(left, upper, layer, blocks, order, rows, chips):
     depth = left.shape[1] // 2
-    span = blocks[0].shape[1] * rows
+    count = len(blocks) // PARTS
+    span = blocks[0].shape[1] * count
     share = left.shape[0] // chips
     whole = [pl.BlockSpec(b.shape, lambda k, s: (0, 0, 0)) for b in blocks]
     return pl.pallas_call(
-        functools.partial(product_kernel, rows, rows // 2),
+        functools.partial(product_kernel, rows, rows // 2, count == rows),
         grid_spec=pltpu.PrefetchScalarGridSpec(
             num_scalar_prefetch=1,
             grid=(chips,),
@@ -151,6 +147,107 @@
     )(order, left, upper, *blocks)
 
 
+def panel_kernel(rows, count, groups, parts, row_ref, *refs):
+    shares, refs = refs[: groups * parts], refs[groups * parts :]
+    factors, refs = refs[:count], refs[count:]
+    older, refs = refs[: 2 * (count - 1)], refs[2 * (count - 1) :]
+    high_ref, low_ref, out_ref, sum_ref, factor_high, factor_low = refs
+    width, wide = factors[0].shape[0], factors[0].shape[3]
+
+    @pl.when(pl.program_id(0) == 0)
+    def _():
+        sum_ref[...] = jnp.zeros_like(sum_ref)
+        for n in range(count):
+            for j in range(width):
+                columns = slice(j * wide, (j + 1) * wide)
+                if n or groups == 1:
+                    high, low = halves(factors[n][j, 0])
+                    factor_high[n, :, columns] = high
+                    factor_low[n, :, columns] = low
+                    continue
+                blk = factors[n].shape[2] // rows
+                for step in range(rows):
+                    owner = lax.rem(row_ref[0] + rows - step, rows)
+                    at = pl.ds(pl.multiple_of(owner * blk, blk), blk)
+                    high, low = halves(factors[n][j, 0, at, :])
+                    factor_high[n, step * blk : (step + 1) * blk, columns] = high
+                    factor_low[n, step * blk : (step + 1) * blk, columns] = low
+
+    def dot(a, b):
+        return jnp.dot(a, b, preferred_element_type=jnp.float32)
+
+    sums = []
+    for g in range(groups):
+        total = shares[g * parts][...]
+        for p in range(1, parts):
+            total = total + shares[g * parts + p][...]
+        sums.append(total)
+    total = jnp.concatenate(sums, axis=1) if groups > 1 else sums[0]
+    high, low = halves(total)
+    high_ref[...] = high
+    low_ref[...] = low
+    pairs = [(high, low)] + [
+        (older[2 * n][...], older[2 * n + 1][...]) for n in range(count - 1)
+    ]
+    panel = jnp.zeros((total.shape[0], factor_high.shape[2]), jnp.float32)
+    for n, (high, low) in enumerate(pairs):
+        panel += dot(high, factor_high[n])
+        panel += dot(low, factor_high[n])
+        panel += dot(high, factor_low[n])
+    sum_ref[...] += jnp.sum((panel * panel).reshape(-1, 8, panel.shape[1]), axis=0)
+    out_ref[...] = panel.T.reshape(out_ref.shape)
+
+
+def panel_columns(shares, factor, row, cycle, later, older, rows):
+    groups, parts = len(shares), len(shares[0])
+    shares = [x for group in shares for x in group]
+    own, piece = shares[0].shape
+    span = piece * groups
+    blk = span // rows
+    width = span // factor.shape[3]
+    count = len(later)
+    step = min(own, 128)
+    slab = pl.BlockSpec((step, span), lambda i, s: (i, 0))
+    part = pl.BlockSpec((step, piece), lambda i, s: (i, 0))
+    pieces = [
+        pl.BlockSpec(
+            (width, 1, span, factor.shape[3]), functools.partial(lambda n, i, s: (cycle, n, 0, 0), n)
+        )
+        for n in later
+    ]
+    flat = [x for pair in older for x in pair]
+    return pl.pallas_call(
+        functools.partial(panel_kernel, rows, count, groups, parts),
+        grid_spec=pltpu.PrefetchScalarGridSpec(
+            num_scalar_prefetch=1,
+            grid=(own // step,),
+            in_specs=[part] * len(shares) + pieces + [slab] * len(flat),
+            out_specs=[
+                slab,
+                slab,
+                pl.BlockSpec((1, rows, blk, step), lambda i, s: (0, 0, 0, i)),
+                pl.BlockSpec((8, span), lambda i, s: (0, 0)),
+            ],
+            scratch_shapes=[
+                pltpu.VMEM((count, span, span), jnp.bfloat16),
+                pltpu.VMEM((count, span, span), jnp.bfloat16),
+            ],
+        ),
+        out_shape=[
+            jax.ShapeDtypeStruct((own, span), jnp.bfloat16),
+            jax.ShapeDtypeStruct((own, span), jnp.bfloat16),
+            jax.ShapeDtypeStruct((1, rows, blk, own), jnp.float32),
+            jax.ShapeDtypeStruct((8, span), jnp.float32),
+        ],
+        compiler_params=pltpu.CompilerParams(vmem_limit_bytes=LIMIT),
+        cost_estimate=pl.CostEstimate(
+            flops=6 * count * own * span * span,
+            bytes_accessed=4 * own * span * (len(shares) + count + 2),
+            transcendentals=0,
+        ),
+    )(row[None], *shares, *([factor] * count), *flat)
+
+
 def partner(chip, k, chips):
     return chip ^ k if chips & (chips - 1) == 0 else (chip + k) % chips
 
@@ -179,8 +276,6 @@
     half_rows = rows // 2
     high, place = col // rows, col % rows
     core, chip = col % 2, col // 2
-    share = group * blk
-    span = rows * blk
     planes = inverse_rest.shape[2]
     cuts = [planes * p // PARTS for p in range(PARTS + 1)]
     cycles = list(reversed(range(panel_cycles)))
@@ -212,27 +307,33 @@
     matrix_sq = jnp.sum(matrix * matrix)
     row_early = after(row, matrix_sq)
 
-    def order(cycle, active):
-        active = jnp.logical_and(active, high == cycle % ratio).astype(jnp.int32)
+    def order(chunk, active):
+        cycle, first, count = chunk
+        at = place if count == rows else (row - place) % rows - first
+        active = jnp.logical_and(active, high == cycle % ratio)
+        active = jnp.logical_and(active, jnp.logical_and(at >= 0, at < count))
         return jnp.stack(
-            [row_early, place, active] + [partner(chip, k, chips) for k in range(chips)]
+            [row_early, jnp.clip(at, 0, count - 1), active.astype(jnp.int32)]
+            + [partner(chip, k, chips) for k in range(chips)]
         )
 
-
     swap = [(i, i ^ 1) for i in range(cols)]
-    gone, kept, shared = {}, {}, {}
-    for cycle in cycles:
+    kept, shared = {}, {}
+    chunks = chunks_of(rows, panel_cycles)
+    for chunk in chunks:
+        cycle, first, count = chunk
         layer = cycle // ratio
-        gone = product(left_send, upper, layer, panels[cycle], order(cycle, core == 1), rows, chips)
+        blocks = panels[cycle][first * PARTS : (first + count) * PARTS]
+        gone = product(left_send, upper, layer, blocks, order(chunk, core == 1), rows, chips)
         there = lax.ppermute(gone, "col", swap)
-        kept[cycle] = product(
-            left_keep, upper, layer, panels[cycle], order(cycle, core == 0), rows, chips,
-        )
-        shared[cycle] = [kept[cycle][0] + there[0]]
+        mine = product(left_keep, upper, layer, blocks, order(chunk, core == 0), rows, chips)
+        kept[cycle] = mine
+        added = [mine[k] + there[k] for k in range(chips)]
+        shared[chunk] = [added[0]]
         for k in range(1, chips):
-            shared[cycle].append(
+            shared[chunk].append(
                 lax.ppermute(
-                    kept[cycle][k] + there[k],
+                    added[k],
                     "col",
                     [(i, partner(i // 2, k, chips) * 2 + i % 2) for i in range(cols)],
                 )
@@ -260,22 +361,19 @@
     totals = []
     results = []
     waiting = []
-    width = span // factor.shape[3]
     for cycle in cycles:
-        parts = shared[cycle]
+        parts = [shared[chunk] for chunk in chunks if chunk[0] == cycle]
         if cycle:
             parts = after(parts, kept[cycle - 1])
-        total = sum(parts[1:], parts[0])
         if cycle == 0:
-            total = after(total, results)
-        updates[cycle] = total
-
-        wide = factor[cycle * width : (cycle + 1) * width]
-        out = jnp.zeros((), jnp.float32)
-        for later in reversed(range(cycle, panel_cycles)):
-            out = out + dot_split(wide[:, later], updates[later], "ctw,it->cwi")
-        totals.append(jnp.sum(out * out))
-        out = out.reshape(1, rows, blk, share)
+            parts = after(parts, results)
+
+        later = [cycle] + list(updates)
+        high_part, low_part, out, square = panel_columns(
+            parts, factor, row, cycle, later, list(updates.values()), rows
+        )
+        updates[cycle] = (high_part, low_part)
+        totals.append(jnp.sum(square))
         if cycle == 0:
             rest_sq = jnp.sum(squares_send) + jnp.sum(squares_keep)
             sums = jnp.stack([matrix_sq, rest_sq + sum(totals)])
@@ -293,6 +391,17 @@
     return 0.5 * (balance * matrix[:panel_cycles] - mirrored / balance)
 
 
+def chunks_of(rows, panel_cycles):
+    half = rows // 2
+    chunks = []
+    for cycle in reversed(range(panel_cycles)):
+        if cycle < HALVED:
+            chunks += [(cycle, 0, half), (cycle, half, half)]
+        else:
+            chunks += [(cycle, 0, rows)]
+    return chunks
+
+
 def solution(mesh):
     in_specs = (
         P(None, "row", None, "col"),

time: 738 us -> 671 us (0.909)
  waiting for transfers between devices: 307 us -> 237 us
  matrix products: 28 us -> 0 us
  Pallas kernels: 176 us -> 203 us
  local copies, waits for them, and re-layouts: 23.1 us -> 30.5 us
    ppermute x12 -> x15, waiting for transfers between devices: 108 us -> 59 us  [per_device(): lax.ppermute(added[k], 'col', [(i, partner(i // 2, k, chips) * 2 + i % 2)...]
    dot_general x10 -> x0, matrix products: 28 us -> none  [dot_split(): jnp.einsum(form, left, right, precision=lax.Precision.HIGH, preferred_ele...]
    ppermute x5, starting transfers between devices: 32.4 us -> 5.65 us  [total_over(): lax.ppermute(value, axis, [(i, i ^ bit) for i in range(count)])]
    pallas_call x8 -> x14, Pallas kernels: 142 us -> 168 us  [the longest x10 142 us: product(): pl.pallas_call(functools.partial(product_kernel, rows, rows // 2, count =...]
    ppermute x12 -> x15, starting transfers between devices: 15.6 us -> 33.5 us  [per_device(): lax.ppermute(added[k], 'col', [(i, partner(i // 2, k, chips) * 2 + i % 2)...]
    ppermute x12, waiting for transfers between devices: 14.1 us -> 0.03 us  [mirror(): arrived.append(lax.ppermute(block, ('row', 'col'), pairs))]
    ppermute x24, waiting for transfers between devices: 121 us -> 110 us  [per_device(): held[p] = lax.ppermute(block, 'row', ring)]
    add x8 -> x5, other arithmetic: 26.5 us -> 19.4 us  [per_device(): added = [mine[k] + there[k] for k in range(chips)]]
  transfers between devices with their start and end apart: 59 -> 63, of which waited for: 26 -> 25; matrix products, arithmetic and copies ran while one was open for 9% -> 9% of each run, Pallas kernels for 24% -> 29%
where the time goes in v2:
time: 671 us; the launch traced here: 657 us
  waiting for transfers between devices  237 us (35%)
  Pallas kernels  203 us (30%)
  starting transfers between devices  113 us (17%)
  other arithmetic  54.6 us (8%)
  local copies, waits for them, and re-layouts  30.5 us (5%)
  between operations  20 us (3%)
    pallas_call x10, Pallas kernels, product(): pl.pallas_call(functools.partial(product_kernel, rows, rows // 2, count =...  142 us
    ppermute x24, waiting for transfers between devices, per_device(): held[p] = lax.ppermute(block, 'row', ring)  110 us
    ppermute x15, waiting for transfers between devices, per_device(): lax.ppermute(added[k], 'col', [(i, partner(i // 2, k, chips) * 2 + i % 2)...  59 us
    ppermute x12, starting transfers between devices, mirror(): arrived.append(lax.ppermute(block, ('row', 'col'), pairs))  57.3 us
    all_gather x1, waiting for transfers between devices, per_device(): factor_rows = lax.all_gather(lower_inverse, 'row', axis=1, tiled=True)  50 us
    pallas_call x2, Pallas kernels, split_rows(): pl.pallas_call(split_kernel, grid_spec=pltpu.PrefetchScalarGridSpec(num_s...  34.6 us
    ppermute x15, starting transfers between devices, per_device(): lax.ppermute(added[k], 'col', [(i, partner(i // 2, k, chips) * 2 + i % 2)...  33.5 us
    pallas_call x4, Pallas kernels, panel_columns(): pl.pallas_call(functools.partial(panel_kernel, rows, count, groups, parts...  25.6 us
  transfers between devices with their start and end apart: 63, of which 25 were waited for; matrix products, arithmetic and copies ran while one was open for 9% of the time, Pallas kernels for 29%

profile of v2, /device:TPU:0, one launch (start us, length us, event | category | flops | bytes accessed | tf_op | source)
XLA Modules:
  0.0 657.3 jit_solution(9873519981987441786)
XLA Ops:
  7.3 50.0 %all-gather.4.cloned.1.call-done = f32[4,512,256]{2,1,0:T(8,128)} async-done(((f32[4,128,256]{2,1,0:T(8,128)}), f32[4,512,256]{2,1,0:T(8,128)}) %all-gather.4.cloned.1.call-update) | async-done | bytes 2097168 | tf_op jit(solution)/shard_map/all_gather | solution.py:300
  57.3 2.4 slice_bitcast_fusion
  61.6 13.4 %collective-permute-done.1.refs_3_ = f32[7,128,128]{2,1,0:T(8,128)S(1)} collective-permute-done((f32[7,128,128]{2,1,0:T(8,128)S(1)}, f32[7,128,128]{2,1,0:T(8,128)S(1)}, u32[]{:S(2)}, u32[]{:S(2)}) %collective-permute-start.1) | collective-permute-done | bytes 458784 | tf_op jit(solution)/shard_map/ppermute | solution.py:296
  75.8 9.1 %collective-permute-done.refs_2_ = f32[7,128,128]{2,1,0:T(8,128)S(1)} collective-permute-done((f32[7,128,128]{2,1,0:T(8,128)S(1)}, f32[7,128,128]{2,1,0:T(8,128)S(1)}, u32[]{:S(2)}, u32[]{:S(2)}) %collective-permute-start) | collective-permute-done | bytes 458784 | tf_op jit(solution)/shard_map/ppermute | solution.py:296
  85.6 9.2 %collective-permute-done.3.refs_5_ = f32[7,128,128]{2,1,0:T(8,128)} collective-permute-done((f32[7,128,128]{2,1,0:T(8,128)S(1)}, f32[7,128,128]{2,1,0:T(8,128)}, u32[]{:S(2)}, u32[]{:S(2)}) %collective-permute-start.3) | collective-permute-done | bytes 458784 | tf_op jit(solution)/shard_map/ppermute | solution.py:296
  94.8 9.8 %collective-permute-done.2.refs_4_ = f32[7,128,128]{2,1,0:T(8,128)} collective-permute-done((f32[7,128,128]{2,1,0:T(8,128)S(1)}, f32[7,128,128]{2,1,0:T(8,128)}, u32[]{:S(2)}, u32[]{:S(2)}) %collective-permute-start.2) | collective-permute-done | bytes 458784 | tf_op jit(solution)/shard_map/ppermute | solution.py:296
  104.6 9.7 %collective-permute-done.11.refs_3_ = f32[7,128,128]{2,1,0:T(8,128)S(1)} collective-permute-done((f32[7,128,128]{2,1,0:T(8,128)S(1)}, f32[7,128,128]{2,1,0:T(8,128)S(1)}, u32[]{:S(2)}, u32[]{:S(2)}) %collective-permute-start.11) | collective-permute-done | bytes 458784 | tf_op jit(solution)/shard_map/ppermute | solution.py:296
  115.1 9.0 %collective-permute-done.10.refs_2_ = f32[7,128,128]{2,1,0:T(8,128)S(1)} collective-permute-done((f32[7,128,128]{2,1,0:T(8,128)S(1)}, f32[7,128,128]{2,1,0:T(8,128)S(1)}, u32[]{:S(2)}, u32[]{:S(2)}) %collective-permute-start.10) | collective-permute-done | bytes 458784 | tf_op jit(solution)/shard_map/ppermute | solution.py:296
  125.7 8.3 %collective-permute-done.13.refs_5_ = f32[7,128,128]{2,1,0:T(8,128)S(1)} collective-permute-done((f32[7,128,128]{2,1,0:T(8,128)S(1)}, f32[7,128,128]{2,1,0:T(8,128)S(1)}, u32[]{:S(2)}, u32[]{:S(2)}) %collective-permute-start.13) | collective-permute-done | bytes 458784 | tf_op jit(solution)/shard_map/ppermute | solution.py:296
  134.0 9.8 %collective-permute-done.12.refs_4_ = f32[7,128,128]{2,1,0:T(8,128)S(1)} collective-permute-done((f32[7,128,128]{2,1,0:T(8,128)S(1)}, f32[7,128,128]{2,1,0:T(8,128)S(1)}, u32[]{:S(2)}, u32[]{:S(2)}) %collective-permute-start.12) | collective-permute-done | bytes 458784 | tf_op jit(solution)/shard_map/ppermute | solution.py:296
  144.6 15.9 %multiply_reduce_fusion = f32[]{:T(128)} fusion(f32[32,128,16,128]{3,2,1,0:T(8,128)} %param.5), kind=kLoop, calls=%fused_computation | loop fusion | flops 16777215 | bytes 33554436 | tf_op jit(solution)/shard_map/reduce_sum | solution.py:307
  161.8 17.4 %shard_map.55 = (bf16[2048,3584]{1,0:T(8,128)(2,1)}, f32[16,8,128]{2,1,0:T(8,128)S(1)}) custom-call(s32[1]{0:T(128)} %bitcast.1.which_ref, f32[32,14,128,128]{3,2,1,0:T(8,128)} %bitcast.165), custom_call_target="tpu_custom_call" | custom-call | flops 29360128 | bytes 29360128 | tf_op jit(solution)/shard_map/pallas_call | solution.py:49
  179.9 4.3 collective-permute-start.23
  184.3 17.0 %shard_map.58 = f32[4,512,512]{2,1,0:T(8,128)} custom-call(s32[7]{0:T(128)S(1)} %stack.263.order_ref, bf16[2048,3584]{1,0:T(8,128)(2,1)} %get-tuple-element.55.left_ref, f32[2,2,2,128,128]{4,3,2,1,0:T(8,128)S(1)} %bitcast.145, f32[7,128,128]{2,1,0:T(8,128)S(1)} %copy-done.25, f32[7,128,128]{2,1,0:T(8,128)S(1)} %copy-done.22, f32[7,128,128]{2,1,0:T(8,128)S(1)} %copy-done.31, ...), custom_call_target="tpu_custom_call" | custom-call | flops 11274289152 | bytes 18874368 | tf_op jit(solution)/shard_map/pallas_call | solution.py:121
  201.3 12.8 %collective-permute-done.23.refs_5_ = f32[7,128,128]{2,1,0:T(8,128)S(1)} collective-permute-done((f32[7,128,128]{2,1,0:T(8,128)}, f32[7,128,128]{2,1,0:T(8,128)S(1)}, u32[]{:S(2)}, u32[]{:S(2)}) %collective-permute-start.23) | collective-permute-done | bytes 458784 | tf_op jit(solution)/shard_map/ppermute | solution.py:296
  214.1 9.8 %collective-permute-done.22.refs_4_ = f32[7,128,128]{2,1,0:T(8,128)S(1)} collective-permute-done((f32[7,128,128]{2,1,0:T(8,128)}, f32[7,128,128]{2,1,0:T(8,128)S(1)}, u32[]{:S(2)}, u32[]{:S(2)}) %collective-permute-start.22) | collective-permute-done | bytes 458784 | tf_op jit(solution)/shard_map/ppermute | solution.py:296
  224.0 16.4 %shard_map.61 = f32[4,512,512]{2,1,0:T(8,128)} custom-call(s32[7]{0:T(128)S(1)} %stack.269.order_ref, bf16[2048,3584]{1,0:T(8,128)(2,1)} %get-tuple-element.55.left_ref, f32[2,2,2,128,128]{4,3,2,1,0:T(8,128)S(1)} %bitcast.146, f32[7,128,128]{2,1,0:T(8,128)S(1)} %get-tuple-element.56.refs_0_, f32[7,128,128]{2,1,0:T(8,128)S(1)} %get-tuple-element.57.refs_1_, ...), custom_call_target="tpu_custom_call" | custom-call | flops 11274289152 | bytes 18874368 | tf_op jit(solution)/shard_map/pallas_call | solution.py:121
  240.9 16.7 %shard_map.64 = f32[4,512,512]{2,1,0:T(8,128)} custom-call(s32[7]{0:T(128)S(1)} %stack.263.order_ref, bf16[2048,3584]{1,0:T(8,128)(2,1)} %get-tuple-element.55.left_ref, f32[2,2,2,128,128]{4,3,2,1,0:T(8,128)S(1)} %bitcast.147, f32[7,128,128]{2,1,0:T(8,128)S(1)} %get-tuple-element.63.refs_0_, f32[7,128,128]{2,1,0:T(8,128)S(1)} %get-tuple-element.64.refs_1_, ...), custom_call_target="tpu_custom_call" | custom-call | flops 11274289152 | bytes 18874368 | tf_op jit(solution)/shard_map/pallas_call | solution.py:121
  258.5 2.9 collective-permute-start.30
  261.8 17.2 %shard_map.56 = (bf16[2048,3584]{1,0:T(8,128)(2,1)}, f32[16,8,128]{2,1,0:T(8,128)S(1)}) custom-call(s32[1]{0:T(128)} %bitcast.3.which_ref, f32[32,14,128,128]{3,2,1,0:T(8,128)} %bitcast.166), custom_call_target="tpu_custom_call" | custom-call | flops 29360128 | bytes 29360128 | tf_op jit(solution)/shard_map/pallas_call | solution.py:49
  282.3 10.2 %shard_map.68 = f32[4,512,256]{2,1,0:T(8,128)S(1)} custom-call(s32[7]{0:T(128)S(1)} %stack.280.order_ref, bf16[2048,3584]{1,0:T(8,128)(2,1)} %get-tuple-element.55.left_ref, f32[2,2,2,128,128]{4,3,2,1,0:T(8,128)S(1)} %bitcast.148, f32[7,128,128]{2,1,0:T(8,128)S(1)} %get-tuple-element.72.refs_0_, f32[7,128,128]{2,1,0:T(8,128)S(1)} %get-tuple-element.73.refs_1_, ...), custom_call_target="tpu_custom_call" | custom-call | flops 5637144576 | bytes 16777216 | tf_op jit(solution)/shard_map/pallas_call | solution.py:121
  293.8 17.2 %shard_map.57 = f32[4,512,512]{2,1,0:T(8,128)} custom-call(s32[7]{0:T(128)S(1)} %stack.260.order_ref, bf16[2048,3584]{1,0:T(8,128)(2,1)} %get-tuple-element.54.left_ref, f32[2,2,2,128,128]{4,3,2,1,0:T(8,128)S(1)} %bitcast.149, f32[7,128,128]{2,1,0:T(8,128)S(1)} %copy-done.26, f32[7,128,128]{2,1,0:T(8,128)S(1)} %copy-done.23, f32[7,128,128]{2,1,0:T(8,128)S(1)} %copy-done.32, ...), custom_call_target="tpu_custom_call" | custom-call | flops 11274289152 | bytes 18874368 | tf_op jit(solution)/shard_map/pallas_call | solution.py:121
  311.4 16.8 %shard_map.59 = f32[4,512,512]{2,1,0:T(8,128)} custom-call(s32[7]{0:T(128)S(1)} %stack.266.order_ref, bf16[2048,3584]{1,0:T(8,128)(2,1)} %get-tuple-element.54.left_ref, f32[2,2,2,128,128]{4,3,2,1,0:T(8,128)S(1)} %bitcast.150, f32[7,128,128]{2,1,0:T(8,128)S(1)} %get-tuple-element.56.refs_0_, f32[7,128,128]{2,1,0:T(8,128)S(1)} %get-tuple-element.57.refs_1_, ...), custom_call_target="tpu_custom_call" | custom-call | flops 11274289152 | bytes 18874368 | tf_op jit(solution)/shard_map/pallas_call | solution.py:121
  329.2 2.2 collective-permute-start.34
  331.4 4.5 fusion.10
  335.9 2.4 collective-permute-start.9
  338.3 4.4 fusion.6
  344.8 7.3 %collective-permute-done.34.refs_2_ = f32[7,128,128]{2,1,0:T(8,128)S(1)} collective-permute-done((f32[7,128,128]{2,1,0:T(8,128)S(1)}, f32[7,128,128]{2,1,0:T(8,128)S(1)}, u32[]{:S(2)}, u32[]{:S(2)}) %collective-permute-start.34) | collective-permute-done | bytes 458784 | tf_op jit(solution)/shard_map/ppermute | solution.py:296
  355.7 16.8 %shard_map.62 = f32[4,512,512]{2,1,0:T(8,128)} custom-call(s32[7]{0:T(128)S(1)} %stack.260.order_ref, bf16[2048,3584]{1,0:T(8,128)(2,1)} %get-tuple-element.54.left_ref, f32[2,2,2,128,128]{4,3,2,1,0:T(8,128)S(1)} %bitcast.151, f32[7,128,128]{2,1,0:T(8,128)S(1)} %copy-done.20, f32[7,128,128]{2,1,0:T(8,128)S(1)} %copy-done.18, ...), custom_call_target="tpu_custom_call" | custom-call | flops 11274289152 | bytes 18874368 | tf_op jit(solution)/shard_map/pallas_call | solution.py:121
  372.5 11.3 %shard_map.69 = f32[4,512,256]{2,1,0:T(8,128)} custom-call(s32[7]{0:T(128)S(1)} %stack.283.order_ref, bf16[2048,3584]{1,0:T(8,128)(2,1)} %get-tuple-element.55.left_ref, f32[2,2,2,128,128]{4,3,2,1,0:T(8,128)S(1)} %bitcast.152, f32[7,128,128]{2,1,0:T(8,128)S(1)} %collective-permute-done.31.refs_0_, f32[7,128,128]{2,1,0:T(8,128)S(1)} %collective-permute-done.33.refs_1_, ...), custom_call_target="tpu_custom_call" | custom-call | flops 5637144576 | bytes 16777216 | tf_op jit(solution)/shard_map/pallas_call | solution.py:121
  383.7 4.8 fusion.2
  393.5 14.6 %collective-permute-done.19.refs_3_ = f32[512,512]{1,0:T(8,128)S(1)} collective-permute-done((f32[512,512]{1,0:T(8,128)}, f32[512,512]{1,0:T(8,128)S(1)}, u32[]{:S(2)}, u32[]{:S(2)}) %collective-permute-start.19) | collective-permute-done | bytes 1048608 | tf_op jit(solution)/shard_map/ppermute | solution.py:335
  409.6 21.0 %collective-permute-done.18.refs_2_ = f32[512,512]{1,0:T(8,128)S(1)} collective-permute-done((f32[512,512]{1,0:T(8,128)}, f32[512,512]{1,0:T(8,128)S(1)}, u32[]{:S(2)}, u32[]{:S(2)}) %collective-permute-start.18) | collective-permute-done | bytes 1048608 | tf_op jit(solution)/shard_map/ppermute | solution.py:335
  432.1 10.2 %shard_map.67 = f32[4,512,256]{2,1,0:T(8,128)S(1)} custom-call(s32[7]{0:T(128)S(1)} %stack.277.order_ref, bf16[2048,3584]{1,0:T(8,128)(2,1)} %get-tuple-element.54.left_ref, f32[2,2,2,128,128]{4,3,2,1,0:T(8,128)S(1)} %bitcast.153, f32[7,128,128]{2,1,0:T(8,128)S(1)} %copy-done.16, f32[7,128,128]{2,1,0:T(8,128)S(1)} %get-tuple-element.73.refs_1_, ...), custom_call_target="tpu_custom_call" | custom-call | flops 5637144576 | bytes 16777216 | tf_op jit(solution)/shard_map/pallas_call | solution.py:121
  442.3 9.9 %shard_map.65 = f32[4,512,256]{2,1,0:T(8,128)S(1)} custom-call(s32[7]{0:T(128)S(1)} %stack.273.order_ref, bf16[2048,3584]{1,0:T(8,128)(2,1)} %get-tuple-element.54.left_ref, f32[2,2,2,128,128]{4,3,2,1,0:T(8,128)S(1)} %bitcast.154, f32[7,128,128]{2,1,0:T(8,128)S(1)} %collective-permute-done.31.refs_0_, f32[7,128,128]{2,1,0:T(8,128)S(1)} %collective-permute-done.33.refs_1_, ...), custom_call_target="tpu_custom_call" | custom-call | flops 5637144576 | bytes 16777216 | tf_op jit(solution)/shard_map/pallas_call | solution.py:121
  453.6 2.7 fusion.18
  457.3 16.5 %collective-permute-done.28.refs_2_ = f32[512,512]{1,0:T(8,128)} collective-permute-done((f32[512,512]{1,0:T(8,128)}, f32[512,512]{1,0:T(8,128)}, u32[]{:S(2)}, u32[]{:S(2)}) %collective-permute-start.28) | collective-permute-done | bytes 1048608 | tf_op jit(solution)/shard_map/ppermute | solution.py:335
  476.5 4.1 shard_map.60
  480.6 5.6 shard_map.63
  486.3 7.0 %shard_map.66 = (bf16[512,512]{1,0:T(8,128)(2,1)S(1)}, bf16[512,512]{1,0:T(8,128)(2,1)S(1)}, f32[1,4,128,512]{3,2,1,0:T(8,128)S(1)}, f32[8,512]{1,0:T(8,128)S(1)}) custom-call(s32[1]{0:T(128)} %bitcast.4.row_ref, f32[512,512]{1,0:T(8,128)S(1)} %copy-done.1, f32[512,512]{1,0:T(8,128)} %collective-permute-done.27.refs_1_, ...), custom_call_target="tpu_custom_call" | custom-call | flops 2415919104 | bytes 9437184 | tf_op jit(solution)/shard_map/pallas_call | solution.py:219
  494.1 5.7 collective-permute-start.47
  502.4 1.8 collective-permute-start.39
  505.0 1.7 collective-permute-start.48
  506.7 7.2 %collective-permute-start.51 = (f32[2,128,512]{2,1,0:T(8,128)}, f32[2,128,512]{2,1,0:T(8,128)}, u32[]{:S(2)}, u32[]{:S(2)}) collective-permute-start(f32[2,128,512]{2,1,0:T(8,128)} %get-tuple-element.130), channel_id=1, source_target_pairs={{0,24},{1,0},{2,8},{3,16},{4,28},{5,4},{6,12},{7,20},{8,25},{9,1},... | collective-permute-start | bytes 1572872 | tf_op jit(solution)/shard_map/ppermute | solution.py:352
  513.9 9.1 %collective-permute-start.50 = (f32[2,128,512]{2,1,0:T(8,128)}, f32[2,128,512]{2,1,0:T(8,128)}, u32[]{:S(2)}, u32[]{:S(2)}) collective-permute-start(f32[2,128,512]{2,1,0:T(8,128)} %get-tuple-element.131), channel_id=1, source_target_pairs={{0,16},{1,24},{2,0},{3,8},{4,20},{5,28},{6,4},{7,12},{8,17},{9,25}... | collective-permute-start | bytes 1572872 | tf_op jit(solution)/shard_map/ppermute | solution.py:352
  523.0 23.8 %collective-permute-start.49 = (f32[2,128,512]{2,1,0:T(8,128)S(1)}, f32[2,128,512]{2,1,0:T(8,128)}, u32[]{:S(2)}, u32[]{:S(2)}) collective-permute-start(f32[2,128,512]{2,1,0:T(8,128)S(1)} %get-tuple-element.132), channel_id=1, source_target_pairs={{0,8},{1,16},{2,24},{3,0},{4,12},{5,20},{6,28},{7,4},{8,9},{9,17},... | collective-permute-start | bytes 1572872 | tf_op jit(solution)/shard_map/ppermute | solution.py:352
  546.8 3.0 fusion.14
  558.8 10.3 %collective-permute-start.43 = (f32[512,256]{1,0:T(8,128)}, f32[512,256]{1,0:T(8,128)}, u32[]{:S(2)}, u32[]{:S(2)}) collective-permute-start(f32[512,256]{1,0:T(8,128)} %get-tuple-element.109), channel_id=1, source_target_pairs={{0,6},{1,7},{2,4},{3,5},{4,2},{5,3},{6,0},{7,1},{8,14},{9,15},{10,... | collective-permute-start | bytes 1572872 | tf_op jit(solution)/shard_map/ppermute | solution.py:335
  569.9 4.8 collective-permute-start.41
  574.7 2.0 pad_maximum_fusion.3
  576.7 2.6 reshape.49
  582.6 3.2 pad_maximum_fusion.1
  585.8 3.1 reshape.50
  588.9 6.7 %collective-permute-done.41.refs_5_ = f32[512,256]{1,0:T(8,128)} collective-permute-done((f32[512,256]{1,0:T(8,128)}, f32[512,256]{1,0:T(8,128)}, u32[]{:S(2)}, u32[]{:S(2)}) %collective-permute-start.41) | collective-permute-done | bytes 524320 | tf_op jit(solution)/shard_map/ppermute | solution.py:335
  595.6 8.9 %shard_map.70 = (bf16[512,512]{1,0:T(8,128)(2,1)}, bf16[512,512]{1,0:T(8,128)(2,1)}, f32[1,4,128,512]{3,2,1,0:T(8,128)}, f32[8,512]{1,0:T(8,128)S(1)}) custom-call(s32[1]{0:T(128)} %bitcast.4.row_ref, f32[512,256]{1,0:T(8,128)S(1)} %copy-done.4, f32[512,256]{1,0:T(8,128)S(1)} %collective-permute-done.37.refs_1_, ...), custom_call_target="tpu_custom_call" | custom-call | flops 3221225472 | bytes 14680064 | tf_op jit(solution)/shard_map/pallas_call | solution.py:219
  608.1 2.3 collective-permute-done.52
  610.4 1.7 collective-permute-start.53
  612.2 2.8 collective-permute-done.53
  617.0 4.2 collective-permute-start.60
  621.2 2.0 collective-permute-start.59
  626.4 8.8 %collective-permute-done.55 = f32[2,8,128]{2,1,0:T(8,128)S(1)} collective-permute-done((f32[2,8,128]{2,1,0:T(8,128)S(1)}, f32[2,8,128]{2,1,0:T(8,128)S(1)}, u32[]{:S(2)}, u32[]{:S(2)}) %collective-permute-start.55) | collective-permute-done | bytes 8224 | tf_op jit(solution)/shard_map/ppermute | solution.py:260
  636.9 2.0 collective-permute-done.56
  641.9 2.0 pad_maximum_fusion.5
  645.6 4.5 fusion.1
  (278 shorter events, 62.5 us)
Async XLA Ops:
  6.5 50.8 %all-gather.4.cloned.1.call-start = ((), (), s32[]{:S(2)}) async-start(), calls=%async_computation | async-start | bytes 2621440 | tf_op jit(solution)/shard_map/all_gather | solution.py:300
  7.3 466.8 %all-gather.6.cloned.1.call-start = ((), (), s32[]{:S(2)}) async-start(), calls=%async_computation.1 | async-start | bytes 18874368 | tf_op jit(solution)/shard_map/all_gather | solution.py:301
  59.8 222.5 %copy-start.15 = (f32[7,128,128]{2,1,0:T(8,128)}, f32[7,128,128]{2,1,0:T(8,128)S(1)}, u32[]{:S(2)}) copy-start(f32[7,128,128]{2,1,0:T(8,128)S(1)} %get-tuple-element.72.refs_0_) | copy-start | bytes 1376260
  59.8 15.2 %collective-permute-start.1 = (f32[7,128,128]{2,1,0:T(8,128)S(1)}, f32[7,128,128]{2,1,0:T(8,128)S(1)}, u32[]{:S(2)}, u32[]{:S(2)}) collective-permute-start(f32[7,128,128]{2,1,0:T(8,128)S(1)} %get-tuple-element.123.refs_1_), channel_id=1, source_target_pairs={{0,8},{8,16},{16,24},{24,0},{1,9},{9,17},{17,25},{25,1},{2,10},{10... | collective-permute-start | bytes 1376264 | tf_op jit(solution)/shard_map/ppermute | solution.py:296
  60.0 24.8 %collective-permute-start = (f32[7,128,128]{2,1,0:T(8,128)S(1)}, f32[7,128,128]{2,1,0:T(8,128)S(1)}, u32[]{:S(2)}, u32[]{:S(2)}) collective-permute-start(f32[7,128,128]{2,1,0:T(8,128)S(1)} %get-tuple-element.124.refs_0_), channel_id=1, source_target_pairs={{0,8},{8,16},{16,24},{24,0},{1,9},{9,17},{17,25},{25,1},{2,10},{10... | collective-permute-start | bytes 1376264 | tf_op jit(solution)/shard_map/ppermute | solution.py:296
  75.0 19.8 %collective-permute-start.3 = (f32[7,128,128]{2,1,0:T(8,128)S(1)}, f32[7,128,128]{2,1,0:T(8,128)}, u32[]{:S(2)}, u32[]{:S(2)}) collective-permute-start(f32[7,128,128]{2,1,0:T(8,128)S(1)} %collective-permute-done.1.refs_3_), channel_id=1, source_target_pairs={{0,8},{8,16},{16,24},{24,0},{1,9},{9,17},{17,25},{25,1},{2,10},{10... | collective-permute-start | bytes 1376264 | tf_op jit(solution)/shard_map/ppermute | solution.py:296
  84.8 19.8 %collective-permute-start.2 = (f32[7,128,128]{2,1,0:T(8,128)S(1)}, f32[7,128,128]{2,1,0:T(8,128)}, u32[]{:S(2)}, u32[]{:S(2)}) collective-permute-start(f32[7,128,128]{2,1,0:T(8,128)S(1)} %collective-permute-done.refs_2_), channel_id=1, source_target_pairs={{0,8},{8,16},{16,24},{24,0},{1,9},{9,17},{17,25},{25,1},{2,10},{10... | collective-permute-start | bytes 1376264 | tf_op jit(solution)/shard_map/ppermute | solution.py:296
  94.8 19.6 %collective-permute-start.11 = (f32[7,128,128]{2,1,0:T(8,128)S(1)}, f32[7,128,128]{2,1,0:T(8,128)S(1)}, u32[]{:S(2)}, u32[]{:S(2)}) collective-permute-start(f32[7,128,128]{2,1,0:T(8,128)S(1)} %get-tuple-element.57.refs_1_), channel_id=1, source_target_pairs={{0,8},{8,16},{16,24},{24,0},{1,9},{9,17},{17,25},{25,1},{2,10},{10... | collective-permute-start | bytes 1376264 | tf_op jit(solution)/shard_map/ppermute | solution.py:296
  104.6 19.6 %collective-permute-start.10 = (f32[7,128,128]{2,1,0:T(8,128)S(1)}, f32[7,128,128]{2,1,0:T(8,128)S(1)}, u32[]{:S(2)}, u32[]{:S(2)}) collective-permute-start(f32[7,128,128]{2,1,0:T(8,128)S(1)} %get-tuple-element.56.refs_0_), channel_id=1, source_target_pairs={{0,8},{8,16},{16,24},{24,0},{1,9},{9,17},{17,25},{25,1},{2,10},{10... | collective-permute-start | bytes 1376264 | tf_op jit(solution)/shard_map/ppermute | solution.py:296
  114.3 19.7 %collective-permute-start.13 = (f32[7,128,128]{2,1,0:T(8,128)S(1)}, f32[7,128,128]{2,1,0:T(8,128)S(1)}, u32[]{:S(2)}, u32[]{:S(2)}) collective-permute-start(f32[7,128,128]{2,1,0:T(8,128)S(1)} %collective-permute-done.11.refs_3_), channel_id=1, source_target_pairs={{0,8},{8,16},{16,24},{24,0},{1,9},{9,17},{17,25},{25,1},{2,10},{10... | collective-permute-start | bytes 1376264 | tf_op jit(solution)/shard_map/ppermute | solution.py:296
  124.2 19.7 %collective-permute-start.12 = (f32[7,128,128]{2,1,0:T(8,128)S(1)}, f32[7,128,128]{2,1,0:T(8,128)S(1)}, u32[]{:S(2)}, u32[]{:S(2)}) collective-permute-start(f32[7,128,128]{2,1,0:T(8,128)S(1)} %collective-permute-done.10.refs_2_), channel_id=1, source_target_pairs={{0,8},{8,16},{16,24},{24,0},{1,9},{9,17},{17,25},{25,1},{2,10},{10... | collective-permute-start | bytes 1376264 | tf_op jit(solution)/shard_map/ppermute | solution.py:296
  124.9 54.3 %collective-permute-start.5 = (f32[7,128,128]{2,1,0:T(8,128)}, f32[7,128,128]{2,1,0:T(8,128)}, u32[]{:S(2)}, u32[]{:S(2)}) collective-permute-start(f32[7,128,128]{2,1,0:T(8,128)} %collective-permute-done.3.refs_5_), channel_id=1, source_target_pairs={{0,8},{8,16},{16,24},{24,0},{1,9},{9,17},{17,25},{25,1},{2,10},{10... | collective-permute-start | bytes 1376264 | tf_op jit(solution)/shard_map/ppermute | solution.py:296
  124.9 59.3 %collective-permute-start.4 = (f32[7,128,128]{2,1,0:T(8,128)}, f32[7,128,128]{2,1,0:T(8,128)}, u32[]{:S(2)}, u32[]{:S(2)}) collective-permute-start(f32[7,128,128]{2,1,0:T(8,128)} %collective-permute-done.2.refs_4_), channel_id=1, source_target_pairs={{0,8},{8,16},{16,24},{24,0},{1,9},{9,17},{17,25},{25,1},{2,10},{10... | collective-permute-start | bytes 1376264 | tf_op jit(solution)/shard_map/ppermute | solution.py:296
  134.0 45.9 %collective-permute-start.21 = (f32[7,128,128]{2,1,0:T(8,128)S(1)}, f32[7,128,128]{2,1,0:T(8,128)}, u32[]{:S(2)}, u32[]{:S(2)}) collective-permute-start(f32[7,128,128]{2,1,0:T(8,128)S(1)} %get-tuple-element.64.refs_1_), channel_id=1, source_target_pairs={{0,8},{8,16},{16,24},{24,0},{1,9},{9,17},{17,25},{25,1},{2,10},{10... | collective-permute-start | bytes 1376264 | tf_op jit(solution)/shard_map/ppermute | solution.py:296
  144.6 39.6 %collective-permute-start.20 = (f32[7,128,128]{2,1,0:T(8,128)S(1)}, f32[7,128,128]{2,1,0:T(8,128)}, u32[]{:S(2)}, u32[]{:S(2)}) collective-permute-start(f32[7,128,128]{2,1,0:T(8,128)S(1)} %get-tuple-element.63.refs_0_), channel_id=1, source_target_pairs={{0,8},{8,16},{16,24},{24,0},{1,9},{9,17},{17,25},{25,1},{2,10},{10... | collective-permute-start | bytes 1376264 | tf_op jit(solution)/shard_map/ppermute | solution.py:296
  179.2 44.7 %collective-permute-start.15 = (f32[7,128,128]{2,1,0:T(8,128)S(1)}, f32[7,128,128]{2,1,0:T(8,128)S(1)}, u32[]{:S(2)}, u32[]{:S(2)}) collective-permute-start(f32[7,128,128]{2,1,0:T(8,128)S(1)} %copy-done.40), channel_id=1, source_target_pairs={{0,8},{8,16},{16,24},{24,0},{1,9},{9,17},{17,25},{25,1},{2,10},{10... | collective-permute-start | bytes 1376264 | tf_op jit(solution)/shard_map/ppermute | solution.py:296
  179.3 44.7 %collective-permute-start.14 = (f32[7,128,128]{2,1,0:T(8,128)S(1)}, f32[7,128,128]{2,1,0:T(8,128)S(1)}, u32[]{:S(2)}, u32[]{:S(2)}) collective-permute-start(f32[7,128,128]{2,1,0:T(8,128)S(1)} %copy-done.43), channel_id=1, source_target_pairs={{0,8},{8,16},{16,24},{24,0},{1,9},{9,17},{17,25},{25,1},{2,10},{10... | collective-permute-start | bytes 1376264 | tf_op jit(solution)/shard_map/ppermute | solution.py:296
  179.9 34.2 %collective-permute-start.23 = (f32[7,128,128]{2,1,0:T(8,128)}, f32[7,128,128]{2,1,0:T(8,128)S(1)}, u32[]{:S(2)}, u32[]{:S(2)}) collective-permute-start(f32[7,128,128]{2,1,0:T(8,128)} %collective-permute-done.21.refs_3_), channel_id=1, source_target_pairs={{0,8},{8,16},{16,24},{24,0},{1,9},{9,17},{17,25},{25,1},{2,10},{10... | collective-permute-start | bytes 1376264 | tf_op jit(solution)/shard_map/ppermute | solution.py:296
  184.2 39.7 %collective-permute-start.22 = (f32[7,128,128]{2,1,0:T(8,128)}, f32[7,128,128]{2,1,0:T(8,128)S(1)}, u32[]{:S(2)}, u32[]{:S(2)}) collective-permute-start(f32[7,128,128]{2,1,0:T(8,128)} %collective-permute-done.20.refs_2_), channel_id=1, source_target_pairs={{0,8},{8,16},{16,24},{24,0},{1,9},{9,17},{17,25},{25,1},{2,10},{10... | collective-permute-start | bytes 1376264 | tf_op jit(solution)/shard_map/ppermute | solution.py:296
  201.3 127.9 %collective-permute-start.6 = (f32[4,512,512]{2,1,0:T(8,128)}, f32[4,512,512]{2,1,0:T(8,128)}, u32[]{:S(2)}, u32[]{:S(2)}) collective-permute-start(f32[4,512,512]{2,1,0:T(8,128)} %shard_map.58), channel_id=1, source_target_pairs={{0,1},{1,0},{2,3},{3,2},{4,5},{5,4},{6,7},{7,6},{8,9},{9,8},{10,11... | collective-permute-start | bytes 12582920 | tf_op jit(solution)/shard_map/ppermute | solution.py:328
  214.1 26.3 %collective-permute-start.25 = (f32[7,128,128]{2,1,0:T(8,128)S(1)}, f32[7,128,128]{2,1,0:T(8,128)S(1)}, u32[]{:S(2)}, u32[]{:S(2)}) collective-permute-start(f32[7,128,128]{2,1,0:T(8,128)S(1)} %collective-permute-done.23.refs_5_), channel_id=1, source_target_pairs={{0,8},{8,16},{16,24},{24,0},{1,9},{9,17},{17,25},{25,1},{2,10},{10... | collective-permute-start | bytes 1376264 | tf_op jit(solution)/shard_map/ppermute | solution.py:296
  223.9 16.9 %collective-permute-start.24 = (f32[7,128,128]{2,1,0:T(8,128)S(1)}, f32[7,128,128]{2,1,0:T(8,128)S(1)}, u32[]{:S(2)}, u32[]{:S(2)}) collective-permute-start(f32[7,128,128]{2,1,0:T(8,128)S(1)} %collective-permute-done.22.refs_4_), channel_id=1, source_target_pairs={{0,8},{8,16},{16,24},{24,0},{1,9},{9,17},{17,25},{25,1},{2,10},{10... | collective-permute-start | bytes 1376264 | tf_op jit(solution)/shard_map/ppermute | solution.py:296
  240.4 95.4 %collective-permute-start.16 = (f32[4,512,512]{2,1,0:T(8,128)}, f32[4,512,512]{2,1,0:T(8,128)}, u32[]{:S(2)}, u32[]{:S(2)}) collective-permute-start(f32[4,512,512]{2,1,0:T(8,128)} %shard_map.61), channel_id=1, source_target_pairs={{0,1},{1,0},{2,3},{3,2},{4,5},{5,4},{6,7},{7,6},{8,9},{9,8},{10,11... | collective-permute-start | bytes 12582920 | tf_op jit(solution)/shard_map/ppermute | solution.py:328
  257.5 97.5 %collective-permute-start.26 = (f32[4,512,512]{2,1,0:T(8,128)}, f32[4,512,512]{2,1,0:T(8,128)}, u32[]{:S(2)}, u32[]{:S(2)}) collective-permute-start(f32[4,512,512]{2,1,0:T(8,128)} %shard_map.64), channel_id=1, source_target_pairs={{0,1},{1,0},{2,3},{3,2},{4,5},{5,4},{6,7},{7,6},{8,9},{9,8},{10,11... | collective-permute-start | bytes 12582920 | tf_op jit(solution)/shard_map/ppermute | solution.py:328
  257.7 23.9 %collective-permute-start.32 = (f32[7,128,128]{2,1,0:T(8,128)S(1)}, f32[7,128,128]{2,1,0:T(8,128)}, u32[]{:S(2)}, u32[]{:S(2)}) collective-permute-start(f32[7,128,128]{2,1,0:T(8,128)S(1)} %get-tuple-element.73.refs_1_), channel_id=1, source_target_pairs={{0,8},{8,16},{16,24},{24,0},{1,9},{9,17},{17,25},{25,1},{2,10},{10... | collective-permute-start | bytes 1376264 | tf_op jit(solution)/shard_map/ppermute | solution.py:296
  258.5 23.8 %collective-permute-start.30 = (f32[7,128,128]{2,1,0:T(8,128)S(1)}, f32[7,128,128]{2,1,0:T(8,128)}, u32[]{:S(2)}, u32[]{:S(2)}) collective-permute-start(f32[7,128,128]{2,1,0:T(8,128)S(1)} %get-tuple-element.72.refs_0_), channel_id=1, source_target_pairs={{0,8},{8,16},{16,24},{24,0},{1,9},{9,17},{17,25},{25,1},{2,10},{10... | collective-permute-start | bytes 1376264 | tf_op jit(solution)/shard_map/ppermute | solution.py:296
  292.5 61.1 %collective-permute-start.36 = (f32[4,512,256]{2,1,0:T(8,128)S(1)}, f32[4,512,256]{2,1,0:T(8,128)}, u32[]{:S(2)}, u32[]{:S(2)}) collective-permute-start(f32[4,512,256]{2,1,0:T(8,128)S(1)} %shard_map.68), channel_id=1, source_target_pairs={{0,1},{1,0},{2,3},{3,2},{4,5},{5,4},{6,7},{7,6},{8,9},{9,8},{10,11... | collective-permute-start | bytes 6291464 | tf_op jit(solution)/shard_map/ppermute | solution.py:328
  292.5 18.5 %collective-permute-start.33 = (f32[7,128,128]{2,1,0:T(8,128)}, f32[7,128,128]{2,1,0:T(8,128)S(1)}, u32[]{:S(2)}, u32[]{:S(2)}) collective-permute-start(f32[7,128,128]{2,1,0:T(8,128)} %collective-permute-done.32.refs_3_), channel_id=1, source_target_pairs={{0,8},{8,16},{16,24},{24,0},{1,9},{9,17},{17,25},{25,1},{2,10},{10... | collective-permute-start | bytes 1376264 | tf_op jit(solution)/shard_map/ppermute | solution.py:296
  311.0 17.2 %collective-permute-start.31 = (f32[7,128,128]{2,1,0:T(8,128)}, f32[7,128,128]{2,1,0:T(8,128)S(1)}, u32[]{:S(2)}, u32[]{:S(2)}) collective-permute-start(f32[7,128,128]{2,1,0:T(8,128)} %collective-permute-done.30.refs_2_), channel_id=1, source_target_pairs={{0,8},{8,16},{16,24},{24,0},{1,9},{9,17},{17,25},{25,1},{2,10},{10... | collective-permute-start | bytes 1376264 | tf_op jit(solution)/shard_map/ppermute | solution.py:296
  328.2 15.2 %collective-permute-start.35 = (f32[7,128,128]{2,1,0:T(8,128)S(1)}, f32[7,128,128]{2,1,0:T(8,128)S(1)}, u32[]{:S(2)}, u32[]{:S(2)}) collective-permute-start(f32[7,128,128]{2,1,0:T(8,128)S(1)} %collective-permute-done.33.refs_1_), channel_id=1, source_target_pairs={{0,8},{8,16},{16,24},{24,0},{1,9},{9,17},{17,25},{25,1},{2,10},{10... | collective-permute-start | bytes 1376264 | tf_op jit(solution)/shard_map/ppermute | solution.py:296
  329.2 22.9 %collective-permute-start.34 = (f32[7,128,128]{2,1,0:T(8,128)S(1)}, f32[7,128,128]{2,1,0:T(8,128)S(1)}, u32[]{:S(2)}, u32[]{:S(2)}) collective-permute-start(f32[7,128,128]{2,1,0:T(8,128)S(1)} %collective-permute-done.31.refs_0_), channel_id=1, source_target_pairs={{0,8},{8,16},{16,24},{24,0},{1,9},{9,17},{17,25},{25,1},{2,10},{10... | collective-permute-start | bytes 1376264 | tf_op jit(solution)/shard_map/ppermute | solution.py:296
  335.9 52.7 %collective-permute-start.9 = (f32[512,512]{1,0:T(8,128)}, f32[512,512]{1,0:T(8,128)}, u32[]{:S(2)}, u32[]{:S(2)}) collective-permute-start(f32[512,512]{1,0:T(8,128)} %get-tuple-element.101), channel_id=1, source_target_pairs={{0,6},{1,7},{2,4},{3,5},{4,2},{5,3},{6,0},{7,1},{8,14},{9,15},{10,... | collective-permute-start | bytes 3145736 | tf_op jit(solution)/shard_map/ppermute | solution.py:335
  343.4 45.2 %collective-permute-start.8 = (f32[512,512]{1,0:T(8,128)}, f32[512,512]{1,0:T(8,128)S(1)}, u32[]{:S(2)}, u32[]{:S(2)}) collective-permute-start(f32[512,512]{1,0:T(8,128)} %get-tuple-element.102), channel_id=1, source_target_pairs={{0,4},{1,5},{2,6},{3,7},{4,0},{5,1},{6,2},{7,3},{8,12},{9,13},{10,... | collective-permute-start | bytes 3145736 | tf_op jit(solution)/shard_map/ppermute | solution.py:335
  352.1 38.9 %collective-permute-start.7 = (f32[512,512]{1,0:T(8,128)}, f32[512,512]{1,0:T(8,128)S(1)}, u32[]{:S(2)}, u32[]{:S(2)}) collective-permute-start(f32[512,512]{1,0:T(8,128)} %get-tuple-element.103), channel_id=1, source_target_pairs={{0,2},{1,3},{2,0},{3,1},{4,6},{5,7},{6,4},{7,5},{8,10},{9,11},{10,... | collective-permute-start | bytes 3145736 | tf_op jit(solution)/shard_map/ppermute | solution.py:335
  353.6 54.5 %collective-permute-start.19 = (f32[512,512]{1,0:T(8,128)}, f32[512,512]{1,0:T(8,128)S(1)}, u32[]{:S(2)}, u32[]{:S(2)}) collective-permute-start(f32[512,512]{1,0:T(8,128)} %get-tuple-element.105), channel_id=1, source_target_pairs={{0,6},{1,7},{2,4},{3,5},{4,2},{5,3},{6,0},{7,1},{8,14},{9,15},{10,... | collective-permute-start | bytes 3145736 | tf_op jit(solution)/shard_map/ppermute | solution.py:335
  355.1 75.5 %collective-permute-start.18 = (f32[512,512]{1,0:T(8,128)}, f32[512,512]{1,0:T(8,128)S(1)}, u32[]{:S(2)}, u32[]{:S(2)}) collective-permute-start(f32[512,512]{1,0:T(8,128)} %get-tuple-element.106), channel_id=1, source_target_pairs={{0,4},{1,5},{2,6},{3,7},{4,0},{5,1},{6,2},{7,3},{8,12},{9,13},{10,... | collective-permute-start | bytes 3145736 | tf_op jit(solution)/shard_map/ppermute | solution.py:335
  388.5 113.9 %collective-permute-start.40 = (f32[4,512,256]{2,1,0:T(8,128)}, f32[4,512,256]{2,1,0:T(8,128)}, u32[]{:S(2)}, u32[]{:S(2)}) collective-permute-start(f32[4,512,256]{2,1,0:T(8,128)} %shard_map.69), channel_id=1, source_target_pairs={{0,1},{1,0},{2,3},{3,2},{4,5},{5,4},{6,7},{7,6},{8,9},{9,8},{10,11... | collective-permute-start | bytes 6291464 | tf_op jit(solution)/shard_map/ppermute | solution.py:328
  389.5 66.8 %collective-permute-start.17 = (f32[512,512]{1,0:T(8,128)}, f32[512,512]{1,0:T(8,128)S(1)}, u32[]{:S(2)}, u32[]{:S(2)}) collective-permute-start(f32[512,512]{1,0:T(8,128)} %get-tuple-element.107), channel_id=1, source_target_pairs={{0,2},{1,3},{2,0},{3,1},{4,6},{5,7},{6,4},{7,5},{8,10},{9,11},{10,... | collective-permute-start | bytes 3145736 | tf_op jit(solution)/shard_map/ppermute | solution.py:335
  392.0 65.3 %collective-permute-start.29 = (f32[512,512]{1,0:T(8,128)}, f32[512,512]{1,0:T(8,128)}, u32[]{:S(2)}, u32[]{:S(2)}) collective-permute-start(f32[512,512]{1,0:T(8,128)} %get-tuple-element.97), channel_id=1, source_target_pairs={{0,6},{1,7},{2,4},{3,5},{4,2},{5,3},{6,0},{7,1},{8,14},{9,15},{10,... | collective-permute-start | bytes 3145736 | tf_op jit(solution)/shard_map/ppermute | solution.py:335
  408.1 65.7 %collective-permute-start.28 = (f32[512,512]{1,0:T(8,128)}, f32[512,512]{1,0:T(8,128)}, u32[]{:S(2)}, u32[]{:S(2)}) collective-permute-start(f32[512,512]{1,0:T(8,128)} %get-tuple-element.98), channel_id=1, source_target_pairs={{0,4},{1,5},{2,6},{3,7},{4,0},{5,1},{6,2},{7,3},{8,12},{9,13},{10,... | collective-permute-start | bytes 3145736 | tf_op jit(solution)/shard_map/ppermute | solution.py:335
  430.6 43.4 %collective-permute-start.27 = (f32[512,512]{1,0:T(8,128)}, f32[512,512]{1,0:T(8,128)}, u32[]{:S(2)}, u32[]{:S(2)}) collective-permute-start(f32[512,512]{1,0:T(8,128)} %get-tuple-element.99), channel_id=1, source_target_pairs={{0,2},{1,3},{2,0},{3,1},{4,6},{5,7},{6,4},{7,5},{8,10},{9,11},{10,... | collective-permute-start | bytes 3145736 | tf_op jit(solution)/shard_map/ppermute | solution.py:335
  493.5 10.8 %collective-permute-start.44 = (f32[1,128,512]{2,1,0:T(8,128)S(1)}, f32[1,128,512]{2,1,0:T(8,128)S(1)}, u32[]{:S(2)}, u32[]{:S(2)}) collective-permute-start(f32[1,128,512]{2,1,0:T(8,128)S(1)} %get-tuple-element.145), channel_id=1, source_target_pairs={{0,0},{1,8},{2,16},{3,24},{4,4},{5,12},{6,20},{7,28},{8,1},{9,9},{... | collective-permute-start | bytes 786440 | tf_op jit(solution)/shard_map/ppermute | solution.py:352
  494.1 12.5 %collective-permute-start.47 = (f32[1,128,512]{2,1,0:T(8,128)S(1)}, f32[1,128,512]{2,1,0:T(8,128)S(1)}, u32[]{:S(2)}, u32[]{:S(2)}) collective-permute-start(f32[1,128,512]{2,1,0:T(8,128)S(1)} %get-tuple-element.146), channel_id=1, source_target_pairs={{0,24},{1,0},{2,8},{3,16},{4,28},{5,4},{6,12},{7,20},{8,25},{9,1},... | collective-permute-start | bytes 786440 | tf_op jit(solution)/shard_map/ppermute | solution.py:352
  499.8 14.0 %collective-permute-start.46 = (f32[1,128,512]{2,1,0:T(8,128)S(1)}, f32[1,128,512]{2,1,0:T(8,128)S(1)}, u32[]{:S(2)}, u32[]{:S(2)}) collective-permute-start(f32[1,128,512]{2,1,0:T(8,128)S(1)} %get-tuple-element.147), channel_id=1, source_target_pairs={{0,16},{1,24},{2,0},{3,8},{4,20},{5,28},{6,4},{7,12},{8,17},{9,25}... | collective-permute-start | bytes 786440 | tf_op jit(solution)/shard_map/ppermute | solution.py:352
  499.8 23.1 %collective-permute-start.45 = (f32[1,128,512]{2,1,0:T(8,128)S(1)}, f32[1,128,512]{2,1,0:T(8,128)S(1)}, u32[]{:S(2)}, u32[]{:S(2)}) collective-permute-start(f32[1,128,512]{2,1,0:T(8,128)S(1)} %get-tuple-element.148), channel_id=1, source_target_pairs={{0,8},{1,16},{2,24},{3,0},{4,12},{5,20},{6,28},{7,4},{8,9},{9,17},... | collective-permute-start | bytes 786440 | tf_op jit(solution)/shard_map/ppermute | solution.py:352
  502.4 53.1 %collective-permute-start.39 = (f32[512,256]{1,0:T(8,128)S(1)}, f32[512,256]{1,0:T(8,128)S(1)}, u32[]{:S(2)}, u32[]{:S(2)}) collective-permute-start(f32[512,256]{1,0:T(8,128)S(1)} %get-tuple-element.113), channel_id=1, source_target_pairs={{0,6},{1,7},{2,4},{3,5},{4,2},{5,3},{6,0},{7,1},{8,14},{9,15},{10,... | collective-permute-start | bytes 1572872 | tf_op jit(solution)/shard_map/ppermute | solution.py:335
  505.0 52.2 %collective-permute-start.48 = (f32[2,128,512]{2,1,0:T(8,128)}, f32[2,128,512]{2,1,0:T(8,128)S(1)}, u32[]{:S(2)}, u32[]{:S(2)}) collective-permute-start(f32[2,128,512]{2,1,0:T(8,128)} %get-tuple-element.129), channel_id=1, source_target_pairs={{0,0},{1,8},{2,16},{3,24},{4,4},{5,12},{6,20},{7,28},{8,1},{9,9},{... | collective-permute-start | bytes 1572872 | tf_op jit(solution)/shard_map/ppermute | solution.py:352
  506.7 52.2 %collective-permute-start.51 = (f32[2,128,512]{2,1,0:T(8,128)}, f32[2,128,512]{2,1,0:T(8,128)}, u32[]{:S(2)}, u32[]{:S(2)}) collective-permute-start(f32[2,128,512]{2,1,0:T(8,128)} %get-tuple-element.130), channel_id=1, source_target_pairs={{0,24},{1,0},{2,8},{3,16},{4,28},{5,4},{6,12},{7,20},{8,25},{9,1},... | collective-permute-start | bytes 1572872 | tf_op jit(solution)/shard_map/ppermute | solution.py:352
  513.9 55.2 %collective-permute-start.50 = (f32[2,128,512]{2,1,0:T(8,128)}, f32[2,128,512]{2,1,0:T(8,128)}, u32[]{:S(2)}, u32[]{:S(2)}) collective-permute-start(f32[2,128,512]{2,1,0:T(8,128)} %get-tuple-element.131), channel_id=1, source_target_pairs={{0,16},{1,24},{2,0},{3,8},{4,20},{5,28},{6,4},{7,12},{8,17},{9,25}... | collective-permute-start | bytes 1572872 | tf_op jit(solution)/shard_map/ppermute | solution.py:352
  523.0 47.0 %collective-permute-start.49 = (f32[2,128,512]{2,1,0:T(8,128)S(1)}, f32[2,128,512]{2,1,0:T(8,128)}, u32[]{:S(2)}, u32[]{:S(2)}) collective-permute-start(f32[2,128,512]{2,1,0:T(8,128)S(1)} %get-tuple-element.132), channel_id=1, source_target_pairs={{0,8},{1,16},{2,24},{3,0},{4,12},{5,20},{6,28},{7,4},{8,9},{9,17},... | collective-permute-start | bytes 1572872 | tf_op jit(solution)/shard_map/ppermute | solution.py:352
  555.6 33.3 %collective-permute-start.38 = (f32[512,256]{1,0:T(8,128)}, f32[512,256]{1,0:T(8,128)S(1)}, u32[]{:S(2)}, u32[]{:S(2)}) collective-permute-start(f32[512,256]{1,0:T(8,128)} %get-tuple-element.114), channel_id=1, source_target_pairs={{0,4},{1,5},{2,6},{3,7},{4,0},{5,1},{6,2},{7,3},{8,12},{9,13},{10,... | collective-permute-start | bytes 1572872 | tf_op jit(solution)/shard_map/ppermute | solution.py:335
  558.0 30.9 %collective-permute-start.37 = (f32[512,256]{1,0:T(8,128)}, f32[512,256]{1,0:T(8,128)S(1)}, u32[]{:S(2)}, u32[]{:S(2)}) collective-permute-start(f32[512,256]{1,0:T(8,128)} %get-tuple-element.115), channel_id=1, source_target_pairs={{0,2},{1,3},{2,0},{3,1},{4,6},{5,7},{6,4},{7,5},{8,10},{9,11},{10,... | collective-permute-start | bytes 1572872 | tf_op jit(solution)/shard_map/ppermute | solution.py:335
  558.8 30.1 %collective-permute-start.43 = (f32[512,256]{1,0:T(8,128)}, f32[512,256]{1,0:T(8,128)}, u32[]{:S(2)}, u32[]{:S(2)}) collective-permute-start(f32[512,256]{1,0:T(8,128)} %get-tuple-element.109), channel_id=1, source_target_pairs={{0,6},{1,7},{2,4},{3,5},{4,2},{5,3},{6,0},{7,1},{8,14},{9,15},{10,... | collective-permute-start | bytes 1572872 | tf_op jit(solution)/shard_map/ppermute | solution.py:335
  569.1 19.8 %collective-permute-start.42 = (f32[512,256]{1,0:T(8,128)}, f32[512,256]{1,0:T(8,128)}, u32[]{:S(2)}, u32[]{:S(2)}) collective-permute-start(f32[512,256]{1,0:T(8,128)} %get-tuple-element.110), channel_id=1, source_target_pairs={{0,4},{1,5},{2,6},{3,7},{4,0},{5,1},{6,2},{7,3},{8,12},{9,13},{10,... | collective-permute-start | bytes 1572872 | tf_op jit(solution)/shard_map/ppermute | solution.py:335
  569.9 25.7 %collective-permute-start.41 = (f32[512,256]{1,0:T(8,128)}, f32[512,256]{1,0:T(8,128)}, u32[]{:S(2)}, u32[]{:S(2)}) collective-permute-start(f32[512,256]{1,0:T(8,128)} %get-tuple-element.111), channel_id=1, source_target_pairs={{0,2},{1,3},{2,0},{3,1},{4,6},{5,7},{6,4},{7,5},{8,10},{9,11},{10,... | collective-permute-start | bytes 1572872 | tf_op jit(solution)/shard_map/ppermute | solution.py:335
  606.7 3.7 collective-permute-start.52
  610.4 4.6 collective-permute-start.53
  616.3 24.6 %collective-permute-start.57 = (f32[1,128,512]{2,1,0:T(8,128)S(1)}, f32[1,128,512]{2,1,0:T(8,128)S(1)}, u32[]{:S(2)}, u32[]{:S(2)}) collective-permute-start(f32[1,128,512]{2,1,0:T(8,128)S(1)} %get-tuple-element.137), channel_id=1, source_target_pairs={{0,0},{1,8},{2,16},{3,24},{4,4},{5,12},{6,20},{7,28},{8,1},{9,9},{... | collective-permute-start | bytes 786440 | tf_op jit(solution)/shard_map/ppermute | solution.py:352
  617.0 24.0 %collective-permute-start.60 = (f32[1,128,512]{2,1,0:T(8,128)S(1)}, f32[1,128,512]{2,1,0:T(8,128)S(1)}, u32[]{:S(2)}, u32[]{:S(2)}) collective-permute-start(f32[1,128,512]{2,1,0:T(8,128)S(1)} %get-tuple-element.138), channel_id=1, source_target_pairs={{0,24},{1,0},{2,8},{3,16},{4,28},{5,4},{6,12},{7,20},{8,25},{9,1},... | collective-permute-start | bytes 786440 | tf_op jit(solution)/shard_map/ppermute | solution.py:352
  621.2 19.8 %collective-permute-start.59 = (f32[1,128,512]{2,1,0:T(8,128)S(1)}, f32[1,128,512]{2,1,0:T(8,128)S(1)}, u32[]{:S(2)}, u32[]{:S(2)}) collective-permute-start(f32[1,128,512]{2,1,0:T(8,128)S(1)} %get-tuple-element.139), channel_id=1, source_target_pairs={{0,16},{1,24},{2,0},{3,8},{4,20},{5,28},{6,4},{7,12},{8,17},{9,25}... | collective-permute-start | bytes 786440 | tf_op jit(solution)/shard_map/ppermute | solution.py:352
  623.2 17.8 %collective-permute-start.58 = (f32[1,128,512]{2,1,0:T(8,128)S(1)}, f32[1,128,512]{2,1,0:T(8,128)S(1)}, u32[]{:S(2)}, u32[]{:S(2)}) collective-permute-start(f32[1,128,512]{2,1,0:T(8,128)S(1)} %get-tuple-element.140), channel_id=1, source_target_pairs={{0,8},{1,16},{2,24},{3,0},{4,12},{5,20},{6,28},{7,4},{8,9},{9,17},... | collective-permute-start | bytes 786440 | tf_op jit(solution)/shard_map/ppermute | solution.py:352
  624.4 1.2 collective-permute-start.54
  625.5 9.7 %collective-permute-start.55 = (f32[2,8,128]{2,1,0:T(8,128)S(1)}, f32[2,8,128]{2,1,0:T(8,128)S(1)}, u32[]{:S(2)}, u32[]{:S(2)}) collective-permute-start(f32[2,8,128]{2,1,0:T(8,128)S(1)} %add.337), channel_id=1, source_target_pairs={{0,2},{1,3},{2,0},{3,1},{4,6},{5,7},{6,4},{7,5},{8,10},{9,11},{10,... | collective-permute-start | bytes 24584 | tf_op jit(solution)/shard_map/ppermute | solution.py:260
  635.3 3.7 collective-permute-start.56
  (68 other events, 1534.8 us)
Sparse Core Ops, SparseCore 0:
  8.9 48.3 all-gather.3
  59.2 88.5 all-gather.5
